TPU v7x, 32 devices: a whole 2x2x4 slice. The times are simulated.
32 devices in a mesh: row: 4 (over x, core), col: 4 (over z), head: 2 (over y).
Axes of the slice: x: 2, y: 2, z: 4, core: 2. Of those that a mesh axis runs over, the one named last changes fastest.
Arguments:
- query_map: bfloat16 [64, 128, 3072], P('row', 'col', 'head'), may hold values from -6 to 6
- key_map: bfloat16 [64, 128, 3072], P('row', 'col', 'head'), may hold values from -7 to 7
- value_map: bfloat16 [64, 128, 3072], P('row', 'col', 'head'), may hold values from -6 to 6
- window_mask: int32 [4, 4, 13, 13], P('row', 'col'), may hold values 0 or 1
- tile_radius: int32 [4, 4], P('row', 'col'), may hold values from 3 to 6, as said below
- dilation_per_tile: int32 [4, 4], P('row', 'col'), may hold values from 1 to 3, as said below
- rel_bias: float32 [48, 13, 13], P('head'), may hold values from -4 to 4
- out_weight: bfloat16 [3072, 3072], P('head'), may hold values from -0.109375 to 0.109375
Outputs:
- mixed: bfloat16 [64, 128, 3072], P('row', 'col', 'head')
Inputs may be any that keep to these rules, and one draw needn't show every extreme that they name: `tile_radius`: in each row of tiles, at least one tile has radius 6 and dilation 3. `dilation_per_tile`: in each row of tiles, at least one tile has radius 6 and dilation 3.
All inputs are finite; a program needn't handle non-finite values. No bound on the sum of `window_mask` on one device may be relied on, other than what follows from the above.
Results may differ from a plain program's by a relative error of at most 0.0073.
Values may be sent and summed in bfloat16 or wider, within the bound.
A program may use at most 384 MiB of HBM per device.

v0:
```python
import math

import jax
import jax.numpy as jnp
from jax import lax
from jax.sharding import PartitionSpec as P

HEAD_DIM = 64
RADIUS_MAX = 6
WINDOW = 13
HALO = 18


def shifted(value, axis, steps):
    count = lax.axis_size(axis)
    leading, last = (max(0, -steps), min(count, count - steps))
    return lax.ppermute(value, axis, [(source, source + steps) for source in range(leading, last)])


def column_source(tile_block, shift_by):
    return shifted(tile_block, "col", shift_by)


def from_row(tile_block, shift_by):
    return shifted(tile_block, "row", shift_by)


def from_relay(tile_block, shift_by):
    return shifted(tile_block, "row", shift_by)


def add_cols(tile_block, halo_depth):
    block_width = tile_block.shape[2]
    left_cols = column_source(tile_block[:, :, block_width - halo_depth :], 1)
    right_cols = column_source(tile_block[:, :, :halo_depth], -1)
    return jnp.concatenate([left_cols, tile_block, right_cols], axis=2)


def add_rows(tile_block, halo_depth):
    block_height = tile_block.shape[1]
    spill_rows = halo_depth - block_height
    rows_above = from_row(tile_block, 1)
    rows_below = from_row(tile_block, -1)
    far_above = from_relay(rows_above[:, block_height - spill_rows :], 1)
    far_below = from_relay(rows_below[:, :spill_rows], -1)
    return jnp.concatenate([far_above, rows_above, tile_block, rows_below, far_below], axis=1)


def shards(
    query_map, key_map, value_map, window_mask, tile_radius, dilation_per_tile, rel_bias, out_weight
):
    tile_rows, tile_cols, features_dev = query_map.shape
    heads_dev = features_dev // HEAD_DIM
    halo_depth = HALO
    kv_pair = jnp.stack([key_map, value_map])
    widened_keys = add_cols(add_rows(kv_pair, halo_depth), halo_depth)
    key_span = tile_cols + 2 * halo_depth
    row_anchor = lax.axis_index("row") * tile_rows
    col_anchor = lax.axis_index("col") * tile_cols
    total_rows = tile_rows * lax.axis_size("row")
    total_cols = tile_cols * lax.axis_size("col")
    radius = tile_radius[0, 0]
    dilation = dilation_per_tile[0, 0]
    pattern = window_mask[0, 0]
    col_steps = jnp.arange(WINDOW, dtype=jnp.int32) - RADIUS_MAX
    column = jnp.arange(tile_cols, dtype=jnp.int32)
    key_spots = jnp.arange(key_span, dtype=jnp.int32)
    destination_tiles = column[None, :] + halo_depth + col_steps[:, None] * dilation
    onehot = (key_spots[None, None, :] == destination_tiles[:, :, None]).astype(jnp.float32)
    onehot_half = onehot.astype(jnp.bfloat16)
    col_global = col_anchor + column[None, :] + col_steps[:, None] * dilation
    column_offset = (
        (jnp.abs(col_steps)[:, None] <= radius) & (col_global >= 0) & (col_global < total_cols)
    )
    row_index = jnp.arange(tile_rows, dtype=jnp.int32)
    query_heads = query_map.reshape(tile_rows, tile_cols, heads_dev, HEAD_DIM)
    score_scale = 1.0 / math.sqrt(HEAD_DIM)
    highest = lax.Precision.HIGHEST
    score_list = []
    valid_list = []
    for offset in range(WINDOW):
        row_lift = offset - RADIUS_MAX
        row_start = halo_depth + row_lift * dilation
        key_strip = lax.dynamic_slice_in_dim(widened_keys[0], row_start, tile_rows, 0)
        key_strip = key_strip.reshape(tile_rows, key_span, heads_dev, HEAD_DIM)
        raw_score = jnp.einsum(
            "icnh,iknh->inck", query_heads, key_strip, preferred_element_type=jnp.float32
        )
        picked = jnp.einsum("inck,bck->incb", raw_score, onehot, precision=highest)
        chosen = (pattern[offset] == 1) | (col_steps == 0) & (row_lift == 0)
        row_global = row_anchor + row_index + row_lift * dilation
        row_fine = (abs(row_lift) <= radius) & (row_global >= 0) & (row_global < total_rows)
        col_valid = jnp.transpose(chosen[:, None] & column_offset)
        bias_row = rel_bias[:, offset, :]
        score_list.append(picked * score_scale + bias_row[None, :, None, :])
        valid_list.append(row_fine[:, None, None, None] & col_valid[None, None, :, :])
    scores = jnp.stack(score_list)
    valid_mask = jnp.stack(valid_list)
    peak_score = jnp.max(jnp.where(valid_mask, scores, -1e30), axis=(0, 4), keepdims=True)
    exponent = jnp.where(
        valid_mask, jnp.exp(jnp.where(valid_mask, scores - peak_score, -60.0)), 0.0
    )
    denominator = jnp.sum(exponent, axis=(0, 4), keepdims=True)
    weights = (exponent / denominator).astype(jnp.bfloat16)
    mixed_heads = jnp.zeros((tile_rows, tile_cols, heads_dev, HEAD_DIM), jnp.float32)
    for offset in range(WINDOW):
        row_start = halo_depth + (offset - RADIUS_MAX) * dilation
        values_slab = lax.dynamic_slice_in_dim(widened_keys[1], row_start, tile_rows, 0)
        values_slab = values_slab.reshape(tile_rows, key_span, heads_dev, HEAD_DIM)
        spread = jnp.einsum(
            "incb,bck->inck", weights[offset], onehot_half, preferred_element_type=jnp.float32
        ).astype(jnp.bfloat16)
        mixed_heads = mixed_heads + jnp.einsum(
            "inck,iknh->icnh", spread, values_slab, preferred_element_type=jnp.float32
        )
    attended = mixed_heads.reshape(tile_rows * tile_cols, features_dev).astype(jnp.bfloat16)
    partials = jnp.dot(attended, out_weight, preferred_element_type=jnp.float32)
    partials = partials.reshape(tile_rows, tile_cols, out_weight.shape[1])
    return lax.psum_scatter(partials, "head", scatter_dimension=2, tiled=True).astype(jnp.bfloat16)


def solution(mesh):
    placed = (
        P("row", "col", "head"),
        P("row", "col", "head"),
        P("row", "col", "head"),
        P("row", "col", None, None),
        P("row", "col"),
        P("row", "col"),
        P("head", None, None),
        P("head", None),
    )
    return jax.shard_map(
        shards, mesh=mesh, in_specs=placed, out_specs=P("row", "col", "head"), check_vma=False
    )
```

profile of v0, /device:TPU:0, one launch (start us, length us, event | category | flops | bytes accessed | tf_op | source)
XLA Modules:
  0.0 1193.9 jit_solution(15250712338779425406)
XLA Ops:
  16.6 33.4 %collective-permute-start.1 = (bf16[2,2,32,1536]{3,2,1,0:T(8,128)(2,1)S(1)}, bf16[2,2,32,1536]{3,2,1,0:T(8,128)(2,1)S(1)}, u32[]{:S(2)}, u32[]{:S(2)}) collective-permute-start(bf16[2,2,32,1536]{3,2,1,0:T(8,128)(2,1)S(1)} %slice.221), channel_id=1, source_target_pairs={{0,8},{8,16},{16,24},{1,9},{9,17},{17,25},{2,10},{10,18},{18,26},{... | collective-permute-start | bytes 1179656 | tf_op jit(solution)/shard_map/ppermute | solution.py:17
  59.5 13.7 %copy.129 = bf16[2,52,18,1536]{3,0,2,1:T(2,128)(2,1)} copy(bf16[2,52,18,1536]{3,2,1,0:T(8,128)(2,1)S(1)} %get-tuple-element.33) | data formatting | bytes 11501568 | tf_op jit(solution)/shard_map/slice | solution.py:34
  106.2 90.1 %collective-permute-done.4 = bf16[2,52,18,1536]{3,0,2,1:T(2,128)(2,1)} collective-permute-done((bf16[2,52,18,1536]{3,0,2,1:T(2,128)(2,1)}, bf16[2,52,18,1536]{3,0,2,1:T(2,128)(2,1)}, u32[]{:S(2)}, u32[]{:S(2)}) %collective-permute-start.4) | collective-permute-done | bytes 5750816 | tf_op jit(solution)/shard_map/ppermute | solution.py:17
  203.2 13.9 %collective-permute-done.5 = bf16[2,52,18,1536]{3,0,2,1:T(2,128)(2,1)} collective-permute-done((bf16[2,52,18,1536]{3,0,2,1:T(2,128)(2,1)}, bf16[2,52,18,1536]{3,0,2,1:T(2,128)(2,1)}, u32[]{:S(2)}, u32[]{:S(2)}) %collective-permute-start.5) | collective-permute-done | bytes 5750816 | tf_op jit(solution)/shard_map/ppermute | solution.py:17
  224.0 23.9 %pad_maximum_fusion = bf16[2,52,68,1536]{3,2,1,0:T(8,128)(2,1)} fusion(bf16[2,52,18,1536]{3,2,1,0:T(8,128)(2,1)} %copy.132, bf16[2,52,32,1536]{3,2,1,0:T(8,128)(2,1)} %copy-done, bf16[2,52,18,1536]{3,2,1,0:T(8,128)(2,1)} %copy.131), kind=kLoop, calls=%fused_computation.4 | loop fusion | flops 65175552 | bytes 43450368 | tf_op jit(solution)/shard_map/concatenate | solution.py:36
  268.2 54.7 %constant_dynamic-slice_fusion.10 = (bf16[1,16,68,1536]{3,2,1,0:T(8,128)(2,1)}, bf16[1,16,68,1536]{3,2,1,0:T(8,128)(2,1)}, bf16[1,16,68,1536]{3,2,1,0:T(8,128)(2...) fusion(bf16[1,52,68,1536]{3,2,1,0:T(8,128)(2,1)} %get-tuple-ele, ...), kind=kLoop, calls=%fused_computation.205 | loop fusion | bytes 160432176 | tf_op jit(solution)/shard_map/dynamic_slice | solution.py:108
  511.2 21.7 %bitcast_dynamic-update-slice_fusion.12 = f32[13,16,24,32,13]{2,4,1,3,0:T(8,128)} fusion(f32[16,24,32,68]{3,2,1,0:T(8,128)} %convolution_bitcast_fusion.12, f32[24,13]{0,1:T(8,128)S(1)} %copy-done.31, s32[13,32]{0,1:T(8,128)S(1)} %copy-done.16), kind=kOutput, calls=%fused_computation.58 | convolution fusion | flops 130698880 | bytes 7539552 | tf_op jit(solution)/shard_map/inck,bck->incb/dot_general | solution.py:89
  532.9 21.7 %bitcast_dynamic-update-slice_fusion.11 = f32[13,16,24,32,13]{2,4,1,3,0:T(8,128)} fusion(f32[13,16,24,32,13]{2,4,1,3,0:T(8,128)} %bitcast_dynamic-update-slice_fusion.12, f32[16,24,32,68]{3,2,1,0:T(8,128)} %convolution_bitcast_fusion.11, f32[24,13]{0,1:T(8,128)S(1)} %copy-done.30, s32[13,32]{0,1:T(8,128)S(1)} %copy-done.16), kind=kOutput, calls=%fused_computation.56 | convolution fusion | flops 130698880 | bytes 10488672 | tf_op jit(solution)/shard_map/inck,bck->incb/dot_general | solution.py:89
  554.7 18.6 %bitcast_dynamic-update-slice_fusion.10 = f32[13,16,24,32,13]{2,4,1,3,0:T(8,128)} fusion(f32[13,16,24,32,13]{2,4,1,3,0:T(8,128)} %bitcast_dynamic-update-slice_fusion.11, f32[16,24,32,68]{3,2,1,0:T(8,128)S(1)} %bitcast.357, f32[24,13]{0,1:T(8,128)S(1)} %copy-done.29, s32[13,32]{0,1:T(8,128)S(1)} %copy-done.16), kind=kOutput, calls=%fused_computation.54 | convolution fusion | flops 130698880 | bytes 7539552 | tf_op jit(solution)/shard_map/inck,bck->incb/dot_general | solution.py:89
  573.3 19.0 %bitcast_dynamic-update-slice_fusion.9 = f32[13,16,24,32,13]{2,4,1,3,0:T(8,128)} fusion(f32[13,16,24,32,13]{2,4,1,3,0:T(8,128)} %bitcast_dynamic-update-slice_fusion.10, f32[16,24,32,68]{3,2,1,0:T(8,128)S(1)} %bitcast.359, f32[24,13]{0,1:T(8,128)S(1)} %copy-done.28, s32[13,32]{0,1:T(8,128)S(1)} %copy-done.16), kind=kOutput, calls=%fused_computation.52 | convolution fusion | flops 130698880 | bytes 7539552 | tf_op jit(solution)/shard_map/inck,bck->incb/dot_general | solution.py:89
  592.4 18.8 %bitcast_dynamic-update-slice_fusion.8 = f32[13,16,24,32,13]{2,4,1,3,0:T(8,128)} fusion(f32[13,16,24,32,13]{2,4,1,3,0:T(8,128)} %bitcast_dynamic-update-slice_fusion.9, f32[16,24,32,68]{3,2,1,0:T(8,128)S(1)} %bitcast.361, f32[24,13]{0,1:T(8,128)S(1)} %copy-done.27, s32[13,32]{0,1:T(8,128)S(1)} %copy-done.16), kind=kOutput, calls=%fused_computation.50 | convolution fusion | flops 130698880 | bytes 7539552 | tf_op jit(solution)/shard_map/inck,bck->incb/dot_general | solution.py:89
  611.2 18.9 %bitcast_dynamic-update-slice_fusion.7 = f32[13,16,24,32,13]{2,4,1,3,0:T(8,128)} fusion(f32[13,16,24,32,13]{2,4,1,3,0:T(8,128)} %bitcast_dynamic-update-slice_fusion.8, f32[16,24,32,68]{3,2,1,0:T(8,128)S(1)} %bitcast.363, f32[24,13]{0,1:T(8,128)S(1)} %copy-done.26, s32[13,32]{0,1:T(8,128)S(1)} %copy-done.16), kind=kOutput, calls=%fused_computation.48 | convolution fusion | flops 130698880 | bytes 7539552 | tf_op jit(solution)/shard_map/inck,bck->incb/dot_general | solution.py:89
  630.1 18.9 %bitcast_dynamic-update-slice_fusion.6 = f32[13,16,24,32,13]{2,4,1,3,0:T(8,128)} fusion(f32[13,16,24,32,13]{2,4,1,3,0:T(8,128)} %bitcast_dynamic-update-slice_fusion.7, f32[16,24,32,68]{3,2,1,0:T(8,128)S(1)} %bitcast.365, f32[24,13]{0,1:T(8,128)S(1)} %copy-done.25, s32[13,32]{0,1:T(8,128)S(1)} %copy-done.16), kind=kOutput, calls=%fused_computation.46 | convolution fusion | flops 130698880 | bytes 7539552 | tf_op jit(solution)/shard_map/inck,bck->incb/dot_general | solution.py:89
  649.0 18.8 %bitcast_dynamic-update-slice_fusion.5 = f32[13,16,24,32,13]{2,4,1,3,0:T(8,128)} fusion(f32[13,16,24,32,13]{2,4,1,3,0:T(8,128)} %bitcast_dynamic-update-slice_fusion.6, f32[16,24,32,68]{3,2,1,0:T(8,128)S(1)} %bitcast.367, f32[24,13]{0,1:T(8,128)S(1)} %copy-done.24, s32[13,32]{0,1:T(8,128)S(1)} %copy-done.16), kind=kOutput, calls=%fused_computation.44 | convolution fusion | flops 130698880 | bytes 7539552 | tf_op jit(solution)/shard_map/inck,bck->incb/dot_general | solution.py:89
  667.9 19.1 %bitcast_dynamic-update-slice_fusion.4 = f32[13,16,24,32,13]{2,4,1,3,0:T(8,128)} fusion(f32[13,16,24,32,13]{2,4,1,3,0:T(8,128)} %bitcast_dynamic-update-slice_fusion.5, f32[16,24,32,68]{3,2,1,0:T(8,128)S(1)} %bitcast.369, f32[24,13]{0,1:T(8,128)S(1)} %copy-done.23, s32[13,32]{0,1:T(8,128)S(1)} %copy-done.16), kind=kOutput, calls=%fused_computation.42 | convolution fusion | flops 130698880 | bytes 7539552 | tf_op jit(solution)/shard_map/inck,bck->incb/dot_general | solution.py:89
  687.0 18.8 %bitcast_dynamic-update-slice_fusion.3 = f32[13,16,24,32,13]{2,4,1,3,0:T(8,128)} fusion(f32[13,16,24,32,13]{2,4,1,3,0:T(8,128)} %bitcast_dynamic-update-slice_fusion.4, f32[16,24,32,68]{3,2,1,0:T(8,128)S(1)} %bitcast.371, f32[24,13]{0,1:T(8,128)S(1)} %copy-done.22, s32[13,32]{0,1:T(8,128)S(1)} %copy-done.16), kind=kOutput, calls=%fused_computation.40 | convolution fusion | flops 130698880 | bytes 7539552 | tf_op jit(solution)/shard_map/inck,bck->incb/dot_general | solution.py:89
  705.8 18.8 %bitcast_dynamic-update-slice_fusion.2 = f32[13,16,24,32,13]{2,4,1,3,0:T(8,128)} fusion(f32[13,16,24,32,13]{2,4,1,3,0:T(8,128)} %bitcast_dynamic-update-slice_fusion.3, f32[16,24,32,68]{3,2,1,0:T(8,128)S(1)} %bitcast.373, f32[24,13]{0,1:T(8,128)S(1)} %copy-done.21, s32[13,32]{0,1:T(8,128)S(1)} %copy-done.16), kind=kOutput, calls=%fused_computation.38 | convolution fusion | flops 130698880 | bytes 7539552 | tf_op jit(solution)/shard_map/inck,bck->incb/dot_general | solution.py:89
  724.6 18.7 %bitcast_dynamic-update-slice_fusion.1 = f32[13,16,24,32,13]{2,4,1,3,0:T(8,128)} fusion(f32[13,16,24,32,13]{2,4,1,3,0:T(8,128)} %bitcast_dynamic-update-slice_fusion.2, f32[16,24,32,68]{3,2,1,0:T(8,128)S(1)} %bitcast.375, f32[24,13]{0,1:T(8,128)S(1)} %copy-done.20, s32[13,32]{0,1:T(8,128)S(1)} %copy-done.16), kind=kOutput, calls=%fused_computation.36 | convolution fusion | flops 130698880 | bytes 7539552 | tf_op jit(solution)/shard_map/inck,bck->incb/dot_general | solution.py:89
  743.4 18.9 %bitcast_dynamic-update-slice_fusion = f32[13,16,24,32,13]{2,4,1,3,0:T(8,128)} fusion(f32[13,16,24,32,13]{2,4,1,3,0:T(8,128)} %bitcast_dynamic-update-slice_fusion.1, f32[16,24,32,68]{3,2,1,0:T(8,128)S(1)} %convolution_bitcast_fusion, f32[24,13]{0,1:T(8,128)S(1)} %copy-done.19, s32[13,32]{0,1:T(8,128)S(1)} %copy-done.16), kind=kOutput, calls=%fused_computation.34 | convolution fusion | flops 130698880 | bytes 7539552 | tf_op jit(solution)/shard_map/inck,bck->incb/dot_general | solution.py:89
  762.3 21.8 %select_reduce_fusion = f32[16,24,32]{1,0,2:T(8,128)S(1)} fusion(f32[13,16,24,32,13]{2,4,1,3,0:T(8,128)} %bitcast_dynamic-update-slice_fusion, pred[13,16,32,13]{3,1,2,0:T(8,128)(4,1)S(1)} %copy-done.9), kind=kLoop, calls=%fused_computation.2 | loop fusion | flops 4141056 | bytes 8442368 | tf_op jit(solution)/shard_map/reduce_max | solution.py:99
  784.1 26.5 %fusion = f32[16,24,32]{1,0,2:T(8,128)S(1)} fusion(f32[13,16,24,32,13]{2,4,1,3,0:T(8,128)} %bitcast_dynamic-update-slice_fusion, f32[16,24,32]{1,0,2:T(8,128)S(1)} %select_reduce_fusion, pred[13,16,32,13]{3,1,2,0:T(8,128)(4,1)S(1)} %copy-done.9), kind=kLoop, calls=%fused_computation.3 | loop fusion | flops 8294400 | bytes 8491520 | tf_op jit(solution)/shard_map/reduce_sum | solution.py:103
  810.6 26.0 %divide_convert_fusion = bf16[13,16,24,32,13]{2,4,1,3,0:T(8,128)(2,1)S(1)} fusion(f32[13,16,24,32,13]{2,4,1,3,0:T(8,128)} %bitcast_dynamic-update-slice_fusion, f32[16,24,32]{1,0,2:T(8,128)S(1)} %fusion, f32[16,24,32]{1,0,2:T(8,128)S(1)} %select_reduce_fusion, pred[13,16,32,13]{3,1,2,0:T(8,128)(4,1)S(1)} %copy-done.9), kind=kLoop, calls=%fused_computation | loop fusion | flops 10383360 | bytes 12644864 | tf_op jit(solution)/shard_map/convert_element_type | solution.py:104
  1059.8 28.9 %fusion.55 = bf16[16,32,24,64]{3,1,2,0:T(8,128)(2,1)} fusion(f32[16,24,64,32]{2,3,1,0:T(8,128)} %fusion.29, f32[16,24,64,32]{2,3,1,0:T(8,128)} %fusion.31, f32[16,24,64,32]{2,3,1,0:T(8,128)} %fusion.33, f32[16,24,64,32]{2,3,1,0:T(8,128)} %fusion.35, f32[16,24,64,32]{2,3,1,0:T(8,128)} %fusion.37, f32[16,24,64,32]{2,3,1,0:T(8,128)} %fusion.39, ...), kind=kOutput, calls=%fused_computation.102 | convolution fusion | flops 117178368 | bytes 44335104 | tf_op jit(solution)/shard_map/inck,iknh->icnh/dot_general | solution.py:113
  1104.7 78.8 %reduce-scatter.2.cloned.1.call-done = f32[16,32,1536]{2,1,0:T(8,128)} async-done(((f32[16,32,3072]{2,1,0:T(8,128)}), f32[16,32,1536]{2,1,0:T(8,128)}) %reduce-scatter.2.cloned.1.call-update) | async-done | bytes 3145744 | tf_op jit(solution)/shard_map/reduce_scatter | solution.py:119
  (274 shorter events, 515.6 us)
Async XLA Ops:
  6.5 1177.0 %reduce-scatter.2.cloned.1.call-start = ((), (), s32[]{:S(2)}) async-start(), calls=%async_computation.1 | async-start | bytes 9437184 | tf_op jit(solution)/shard_map/reduce_scatter | solution.py:119
  6.5 45.2 %copy-start.17 = (bf16[16,32,1536]{2,1,0:T(8,128)(2,1)S(1)}, bf16[16,32,1536]{2,1,0:T(8,128)(2,1)}, u32[]{:S(2)}) copy-start(bf16[16,32,1536]{2,1,0:T(8,128)(2,1)} %param.10) | copy-start | bytes 4718596
  6.5 45.2 %copy-start.18 = (bf16[16,32,1536]{2,1,0:T(8,128)(2,1)S(1)}, bf16[16,32,1536]{2,1,0:T(8,128)(2,1)}, u32[]{:S(2)}) copy-start(bf16[16,32,1536]{2,1,0:T(8,128)(2,1)} %param.9) | copy-start | bytes 4718596
  8.9 7.7 collective-permute-start
  11.5 38.6 %collective-permute-start.2 = (bf16[2,16,32,1536]{3,2,1,0:T(8,128)(2,1)S(1)}, bf16[2,16,32,1536]{3,2,1,0:T(8,128)(2,1)S(1)}, u32[]{:S(2)}, u32[]{:S(2)}) collective-permute-start(bf16[2,16,32,1536]{3,2,1,0:T(8,128)(2,1)S(1)} %pad_maximum_fusion.3), channel_id=1, source_target_pairs={{8,0},{16,8},{24,16},{9,1},{17,9},{25,17},{10,2},{18,10},{26,18},{... | collective-permute-start | bytes 9437192 | tf_op jit(solution)/shard_map/ppermute | solution.py:17
  16.6 34.8 %collective-permute-start.1 = (bf16[2,2,32,1536]{3,2,1,0:T(8,128)(2,1)S(1)}, bf16[2,2,32,1536]{3,2,1,0:T(8,128)(2,1)S(1)}, u32[]{:S(2)}, u32[]{:S(2)}) collective-permute-start(bf16[2,2,32,1536]{3,2,1,0:T(8,128)(2,1)S(1)} %slice.221), channel_id=1, source_target_pairs={{0,8},{8,16},{16,24},{1,9},{9,17},{17,25},{2,10},{10,18},{18,26},{... | collective-permute-start | bytes 1179656 | tf_op jit(solution)/shard_map/ppermute | solution.py:17
  50.1 5.6 collective-permute-start.3
  73.2 123.1 %collective-permute-start.4 = (bf16[2,52,18,1536]{3,0,2,1:T(2,128)(2,1)}, bf16[2,52,18,1536]{3,0,2,1:T(2,128)(2,1)}, u32[]{:S(2)}, u32[]{:S(2)}) collective-permute-start(bf16[2,52,18,1536]{3,0,2,1:T(2,128)(2,1)} %copy.129), channel_id=1, source_target_pairs={{0,2},{2,4},{4,6},{1,3},{3,5},{5,7},{8,10},{10,12},{12,14},{9,11},... | collective-permute-start | bytes 17252360 | tf_op jit(solution)/shard_map/ppermute | solution.py:17
  79.1 21.1 %copy-start.32 = (s32[1,1,13,13]{3,1,2,0:T(1,128)S(1)}, s32[1,1,13,13]{3,1,2,0:T(1,128)}, u32[]{:S(2)}) copy-start(s32[1,1,13,13]{3,1,2,0:T(1,128)} %param.11) | copy-start | bytes 2032
  92.8 124.3 %collective-permute-start.5 = (bf16[2,52,18,1536]{3,0,2,1:T(2,128)(2,1)}, bf16[2,52,18,1536]{3,0,2,1:T(2,128)(2,1)}, u32[]{:S(2)}, u32[]{:S(2)}) collective-permute-start(bf16[2,52,18,1536]{3,0,2,1:T(2,128)(2,1)} %copy.130), channel_id=1, source_target_pairs={{2,0},{4,2},{6,4},{3,1},{5,3},{7,5},{10,8},{12,10},{14,12},{11,9},... | collective-permute-start | bytes 17252360 | tf_op jit(solution)/shard_map/ppermute | solution.py:17
  511.2 21.7 %copy-start.30 = (f32[24,13]{0,1:T(8,128)S(1)}, f32[24,13]{0,1:T(8,128)}, u32[]{:S(2)}) copy-start(f32[24,13]{0,1:T(8,128)} %get-tuple-element.45) | copy-start | bytes 3748
  511.2 43.4 %slice-start = ((s8[6291456]{0:T(1024)(128)(4,1)}), s8[4194304]{0:T(1024)(128)(4,1)S(1)}, s32[]{:S(2)}) async-start(s8[6291456]{0:T(1024)(128)(4,1)} %bitcast.356), calls=%async_computation.2 | async-start | bytes 8388608
  532.9 21.7 %copy-start.29 = (f32[24,13]{0,1:T(8,128)S(1)}, f32[24,13]{0,1:T(8,128)}, u32[]{:S(2)}) copy-start(f32[24,13]{0,1:T(8,128)} %get-tuple-element.44) | copy-start | bytes 3748
  532.9 21.7 %slice-start.1 = ((s8[6291456]{0:T(1024)(128)(4,1)}), s8[2097152]{0:T(1024)(128)(4,1)S(1)}, s32[]{:S(2)}) async-start(s8[6291456]{0:T(1024)(128)(4,1)} %bitcast.356), calls=%async_computation.3 | async-start | bytes 4194304
  532.9 40.4 %slice-start.2 = ((s8[6291456]{0:T(1024)(128)(4,1)}), s8[4194304]{0:T(1024)(128)(4,1)S(1)}, s32[]{:S(2)}) async-start(s8[6291456]{0:T(1024)(128)(4,1)} %bitcast.358), calls=%async_computation.4 | async-start | bytes 8388608
  554.6 37.7 %slice-start.4 = ((s8[6291456]{0:T(1024)(128)(4,1)}), s8[4194304]{0:T(1024)(128)(4,1)S(1)}, s32[]{:S(2)}) async-start(s8[6291456]{0:T(1024)(128)(4,1)} %bitcast.360), calls=%async_computation.6 | async-start | bytes 8388608
  573.3 37.8 %slice-start.6 = ((s8[6291456]{0:T(1024)(128)(4,1)}), s8[4194304]{0:T(1024)(128)(4,1)S(1)}, s32[]{:S(2)}) async-start(s8[6291456]{0:T(1024)(128)(4,1)} %bitcast.362), calls=%async_computation.8 | async-start | bytes 8388608
  592.4 37.7 %slice-start.8 = ((s8[6291456]{0:T(1024)(128)(4,1)}), s8[4194304]{0:T(1024)(128)(4,1)S(1)}, s32[]{:S(2)}) async-start(s8[6291456]{0:T(1024)(128)(4,1)} %bitcast.364), calls=%async_computation.10 | async-start | bytes 8388608
  611.2 37.8 %slice-start.10 = ((s8[6291456]{0:T(1024)(128)(4,1)}), s8[4194304]{0:T(1024)(128)(4,1)S(1)}, s32[]{:S(2)}) async-start(s8[6291456]{0:T(1024)(128)(4,1)} %bitcast.366), calls=%async_computation.12 | async-start | bytes 8388608
  630.1 37.8 %slice-start.12 = ((s8[6291456]{0:T(1024)(128)(4,1)}), s8[4194304]{0:T(1024)(128)(4,1)S(1)}, s32[]{:S(2)}) async-start(s8[6291456]{0:T(1024)(128)(4,1)} %bitcast.368), calls=%async_computation.14 | async-start | bytes 8388608
  649.0 38.0 %slice-start.14 = ((s8[6291456]{0:T(1024)(128)(4,1)}), s8[4194304]{0:T(1024)(128)(4,1)S(1)}, s32[]{:S(2)}) async-start(s8[6291456]{0:T(1024)(128)(4,1)} %bitcast.370), calls=%async_computation.16 | async-start | bytes 8388608
  667.9 19.1 %copy-start.22 = (f32[24,13]{0,1:T(8,128)S(1)}, f32[24,13]{0,1:T(8,128)}, u32[]{:S(2)}) copy-start(f32[24,13]{0,1:T(8,128)} %get-tuple-element.37) | copy-start | bytes 3748
  667.9 37.9 %slice-start.16 = ((s8[6291456]{0:T(1024)(128)(4,1)}), s8[4194304]{0:T(1024)(128)(4,1)S(1)}, s32[]{:S(2)}) async-start(s8[6291456]{0:T(1024)(128)(4,1)} %bitcast.372), calls=%async_computation.18 | async-start | bytes 8388608
  687.0 37.6 %slice-start.18 = ((s8[6291456]{0:T(1024)(128)(4,1)}), s8[4194304]{0:T(1024)(128)(4,1)S(1)}, s32[]{:S(2)}) async-start(s8[6291456]{0:T(1024)(128)(4,1)} %bitcast.374), calls=%async_computation.20 | async-start | bytes 8388608
  (50 other events, 671.7 us)
Sparse Core Ops, SparseCore 0:
  1104.9 78.6 reduce-scatter.1
where the time goes:
time: 1200 us; the launch traced here: 1190 us
  matrix products  511 us (43%)
  local copies, waits for them, and re-layouts  315 us (26%)
  waiting for transfers between devices  190 us (16%)
  other arithmetic  116 us (10%)
  starting transfers between devices  46.3 us (4%)
  between operations  15.8 us (1%)
    dot_general x13, matrix products, shards(): picked = jnp.einsum('inck,bck->incb', raw_score, onehot, precision=highest)  251 us
    dynamic_slice x14, local copies, waits for them, and re-layouts, shards(): lax.dynamic_slice_in_dim(widened_keys[1], row_start, tile_rows, 0)  142 us
    dot_general x13, matrix products, shards(): jnp.einsum('inck,iknh->icnh', spread, values_slab, preferred_element_type...  128 us
    ppermute x6, waiting for transfers between devices, shifted(): lax.ppermute(value, axis, [(source, source + steps) for source in range(l...  111 us
    reshape x13, local copies, waits for them, and re-layouts, shards(): key_strip = key_strip.reshape(tile_rows, key_span, heads_dev, HEAD_DIM)  101 us
    dot_general x13, matrix products, shards(): jnp.einsum('icnh,iknh->inck', query_heads, key_strip, preferred_element_t...  86.8 us
    reduce_scatter x1, waiting for transfers between devices, shards(): lax.psum_scatter(partials, 'head', scatter_dimension=2, tiled=True)  78.8 us
    ppermute x6, starting transfers between devices, shifted(): lax.ppermute(value, axis, [(source, source + steps) for source in range(l...  46.3 us
  transfers between devices with their start and end apart: 7, of which 5 were waited for; matrix products, arithmetic and copies ran while one was open for 3% of the time, Pallas kernels for 0%

commit v1 on v0

v1 whole, which is shorter than its diff:
```python
import functools
import math

import jax
import jax.numpy as jnp
from jax import lax
from jax.experimental import pallas as pl
from jax.experimental.pallas import tpu as pltpu
from jax.sharding import PartitionSpec as P

HEAD_DIM = 64
RADIUS_MAX = 6
WINDOW = 13
HALO = 18
GROUP = 4
GROUP_FEATURES = GROUP * HEAD_DIM
MASKED = -1e30


def shifted(value, axis, steps):
    count = lax.axis_size(axis)
    first, last = (max(0, -steps), min(count, count - steps))
    return lax.ppermute(value, axis, [(source, source + steps) for source in range(first, last)])


def widen_cols(block, key_cols):
    width = block.shape[2]
    left = shifted(block[:, :, width - HALO :], "col", 1)
    right = shifted(block[:, :, :HALO], "col", -1)
    return left, right


def widen_rows(block):
    height = block.shape[1]
    spill = HALO - height
    above = shifted(block, "row", 1)
    below = shifted(block, "row", -1)
    far_above = shifted(above[:, height - spill :], "row", 1)
    far_below = shifted(below[:, :spill], "row", -1)
    return jnp.concatenate([far_above, above, block, below, far_below], axis=1)


def attention_kernel(rows, dilation_ref, q_ref, k_ref, v_ref, bias_ref, row_ref, out_ref):
    dilation = dilation_ref[0]
    cols = q_ref.shape[1]
    lane_head = lax.broadcasted_iota(jnp.int32, (cols, GROUP_FEATURES), 1) // HEAD_DIM

    def one_row(i, carry):
        query = q_ref[i] * jnp.bfloat16(1.0 / math.sqrt(HEAD_DIM))
        zero = jnp.zeros_like(query)
        stacked = jnp.concatenate(
            [jnp.where(lane_head == h, query, zero) for h in range(GROUP)], axis=0
        )
        places = [i + HALO + (a - RADIUS_MAX) * dilation for a in range(WINDOW)]
        keys = jnp.concatenate([k_ref[place] for place in places], axis=0)
        scores = lax.dot_general(
            stacked, keys, (((1,), (1,)), ((), ())), preferred_element_type=jnp.float32
        )
        scores = scores + bias_ref[0] + row_ref[pl.ds(i, 1), :]
        peak = jnp.max(scores, axis=1, keepdims=True)
        exponent = jnp.exp(scores - peak)
        total = jnp.sum(exponent, axis=1, keepdims=True)
        values = jnp.concatenate([v_ref[place] for place in places], axis=0)
        summed = jnp.dot(
            exponent.astype(jnp.bfloat16), values, preferred_element_type=jnp.float32
        )
        summed = summed / total
        result = summed[:cols]
        for h in range(1, GROUP):
            result = jnp.where(lane_head == h, summed[h * cols : (h + 1) * cols], result)
        out_ref[i] = result.astype(jnp.bfloat16)
        return carry

    lax.fori_loop(0, rows, one_row, 0)


def attend(dilation, query, keys, values, bias, row_bias, first_group):
    rows, cols, features = query.shape
    groups = features // GROUP_FEATURES
    span_rows, span_cols = keys.shape[:2]
    stacked, depth = bias.shape[1:]
    return pl.pallas_call(
        functools.partial(attention_kernel, rows),
        grid=(groups,),
        in_specs=[
            pl.BlockSpec(memory_space=pltpu.SMEM),
            pl.BlockSpec((rows, cols, GROUP_FEATURES), lambda g: (0, 0, g)),
            pl.BlockSpec((span_rows, span_cols, GROUP_FEATURES), lambda g: (0, 0, g)),
            pl.BlockSpec((span_rows, span_cols, GROUP_FEATURES), lambda g: (0, 0, g)),
            pl.BlockSpec((1, stacked, depth), lambda g: (g + first_group, 0, 0)),
            pl.BlockSpec((rows, depth), lambda g: (0, 0)),
        ],
        out_specs=pl.BlockSpec((rows, cols, GROUP_FEATURES), lambda g: (0, 0, g)),
        out_shape=jax.ShapeDtypeStruct((rows, cols, features), jnp.bfloat16),
        compiler_params=pltpu.CompilerParams(vmem_limit_bytes=40 * 1024 * 1024),
        cost_estimate=pl.CostEstimate(
            flops=groups * rows * 16 * stacked * depth * GROUP_FEATURES,
            bytes_accessed=keys.size * 4,
            transcendentals=groups * rows * stacked * depth,
        ),
    )(dilation, query, keys, values, bias, row_bias)


def bias_tables(rel_bias, pattern, radius, dilation, tile_rows, tile_cols, key_cols):
    heads = rel_bias.shape[0]
    groups = heads // GROUP
    total_rows = tile_rows * lax.axis_size("row")
    total_cols = tile_cols * lax.axis_size("col")
    row_anchor = lax.axis_index("row") * tile_rows
    col_anchor = lax.axis_index("col") * tile_cols
    steps = jnp.arange(WINDOW, dtype=jnp.int32) - RADIUS_MAX
    spot = jnp.arange(key_cols, dtype=jnp.int32)
    offset = jnp.where(
        spot < tile_cols, spot, jnp.where(spot < tile_cols + HALO, spot - tile_cols - HALO, spot - HALO)
    )
    real = spot < tile_cols + 2 * HALO
    column = jnp.arange(tile_cols, dtype=jnp.int32)
    gap = offset[None, :] - column[:, None]
    global_col = col_anchor + offset
    inside = (real & (global_col >= 0) & (global_col < total_cols))[None, :]
    chosen = (pattern == 1) | ((steps[:, None] == 0) & (steps[None, :] == 0))
    chosen = chosen & (jnp.abs(steps)[:, None] <= radius) & (jnp.abs(steps)[None, :] <= radius)
    table = jnp.where(chosen[None], rel_bias, MASKED).reshape(groups, GROUP, 1, WINDOW, WINDOW)
    full = jnp.full((groups, GROUP, tile_cols, WINDOW, key_cols), MASKED, jnp.float32)
    for b in range(WINDOW):
        hit = (gap == (b - RADIUS_MAX) * dilation) & inside
        full = jnp.where(hit[None, None, :, None, :], table[..., b][..., None], full)
    full = full.reshape(groups, GROUP * tile_cols, WINDOW * key_cols)
    row_global = row_anchor + jnp.arange(tile_rows)[:, None] + steps[None, :] * dilation
    row_fine = (row_global >= 0) & (row_global < total_rows)
    row_bias = jnp.where(row_fine, 0.0, MASKED).astype(jnp.float32)
    row_bias = jnp.broadcast_to(row_bias[:, :, None], (tile_rows, WINDOW, key_cols))
    return full, row_bias.reshape(tile_rows, WINDOW * key_cols)


def shards(
    query_map, key_map, value_map, window_mask, tile_radius, dilation_per_tile, rel_bias, out_weight
):
    tile_rows, tile_cols, features = query_map.shape
    key_cols = -(-(tile_cols + 2 * HALO) // 16) * 16
    dilation = dilation_per_tile[0, 0]
    bias, row_bias = bias_tables(
        rel_bias, window_mask[0, 0], tile_radius[0, 0], dilation, tile_rows, tile_cols, key_cols
    )
    groups = features // GROUP_FEATURES
    chunks = 3 if groups % 3 == 0 else 1
    width = features // chunks
    pieces = []
    for c in range(chunks):
        cut = slice(c * width, (c + 1) * width)
        pair = jnp.stack([key_map[..., cut], value_map[..., cut]])
        left, right = widen_cols(pair, key_cols)
        fill = jnp.zeros((2, tile_rows, key_cols - tile_cols - 2 * HALO, width), pair.dtype)
        halo = widen_rows(jnp.concatenate([left, right], axis=2))
        own = widen_rows(pair)
        fill = jnp.zeros((2, own.shape[1], key_cols - tile_cols - 2 * HALO, width), pair.dtype)
        wide = jnp.concatenate([own, halo, fill], axis=2)
        pieces.append(
            attend(
                dilation.reshape(1), query_map[..., cut], wide[0], wide[1], bias, row_bias,
                c * (groups // chunks),
            )
        )
    attended = jnp.concatenate(pieces, axis=2).reshape(tile_rows * tile_cols, features)
    count = lax.axis_size("head")
    model = out_weight.shape[1]
    if count != 2:
        partials = jnp.dot(attended, out_weight, preferred_element_type=jnp.float32)
        mixed = lax.psum_scatter(partials, "head", scatter_dimension=1, tiled=True)
        return mixed.astype(jnp.bfloat16).reshape(tile_rows, tile_cols, model // count)
    me = lax.axis_index("head")
    half = model // 2
    theirs = lax.dynamic_slice_in_dim(out_weight, (1 - me) * half, half, 1)
    mine = lax.dynamic_slice_in_dim(out_weight, me * half, half, 1)
    sent = jnp.dot(attended, theirs, preferred_element_type=jnp.float32).astype(jnp.bfloat16)
    got = lax.ppermute(sent, "head", [(0, 1), (1, 0)])
    kept = jnp.dot(attended, mine, preferred_element_type=jnp.float32)
    mixed = (kept + got.astype(jnp.float32)).astype(jnp.bfloat16)
    return mixed.reshape(tile_rows, tile_cols, half)


def solution(mesh):
    placed = (
        P("row", "col", "head"),
        P("row", "col", "head"),
        P("row", "col", "head"),
        P("row", "col", None, None),
        P("row", "col"),
        P("row", "col"),
        P("head", None, None),
        P("head", None),
    )
    return jax.shard_map(
        shards, mesh=mesh, in_specs=placed, out_specs=P("row", "col", "head"), check_vma=False
    )
```

time: 1200 us -> 519 us (0.43)
  matrix products: 511 us -> 12.1 us
  waiting for transfers between devices: 190 us -> 35.7 us
  Pallas kernels: 0 us -> 77.6 us
  other arithmetic: 116 us -> 44.7 us
  local copies, waits for them, and re-layouts: 315 us -> 244 us
  starting transfers between devices: 46.3 us -> 94.8 us
  between operations: 15.8 us -> 2.74 us
    dot_general x53 -> x2, matrix products: 511 us -> 12.1 us  [the longest x1 6.56 us: shards(): kept = jnp.dot(attended, mine, preferred_element_type=jnp.float32)]
    broadcast_in_dim x1 -> x53, local copies, waits for them, and re-layouts: 2.39 us -> 171 us  [the longest x52 171 us: bias_tables(): jnp.where(hit[None, None, :, None, :], table[..., b][..., None], full)]
    dynamic_slice x14 -> x0, local copies, waits for them, and re-layouts: 142 us -> none  [shards(): lax.dynamic_slice_in_dim(widened_keys[1], row_start, tile_rows, 0)]
    reshape x14 -> x1, local copies, waits for them, and re-layouts: 105 us -> 0.1 us  [bias_tables(): return (full, row_bias.reshape(tile_rows, WINDOW * key_cols))]
    reduce_scatter x1 -> x0, waiting for transfers between devices: 78.8 us -> none  [shards(): lax.psum_scatter(partials, 'head', scatter_dimension=2, tiled=True)]
    pallas_call x0 -> x3, Pallas kernels: none -> 77.6 us  [attend(): pl.pallas_call(functools.partial(attention_kernel, rows), grid=(groups,),...]
    ppermute x6 -> x31, waiting for transfers between devices: 111 us -> 35.7 us  [the longest x1 35.6 us: shards(): got = lax.ppermute(sent, 'head', [(0, 1), (1, 0)])]
    ppermute x6 -> x31, starting transfers between devices: 46.3 us -> 94.8 us  [the longest x30 93.2 us: shifted(): lax.ppermute(value, axis, [(source, source + steps) for source in range(f...]
  transfers between devices with their start and end apart: 7 -> 31, of which waited for: 5 -> 1; matrix products, arithmetic and copies ran while one was open for 3% -> 49% of each run, Pallas kernels for 0% -> 0%
where the time goes in v1:
time: 519 us; the launch traced here: 512 us
  local copies, waits for them, and re-layouts  244 us (47%)
  starting transfers between devices  94.8 us (18%)
  Pallas kernels  77.6 us (15%)
  other arithmetic  44.7 us (9%)
  waiting for transfers between devices  35.7 us (7%)
  matrix products  12.1 us (2%)
    broadcast_in_dim x52, local copies, waits for them, and re-layouts, bias_tables(): jnp.where(hit[None, None, :, None, :], table[..., b][..., None], full)  171 us
    ppermute x30, starting transfers between devices, shifted(): lax.ppermute(value, axis, [(source, source + steps) for source in range(f...  93.2 us
    pallas_call x3, Pallas kernels, attend(): pl.pallas_call(functools.partial(attention_kernel, rows), grid=(groups,),...  77.6 us
    ppermute x1, waiting for transfers between devices, shards(): got = lax.ppermute(sent, 'head', [(0, 1), (1, 0)])  35.6 us
    unnamed x78, local copies, waits for them, and re-layouts  24.7 us
    select_n x1, other arithmetic, bias_tables(): jnp.where(hit[None, None, :, None, :], table[..., b][..., None], full)  17.9 us
    slice x14, local copies, waits for them, and re-layouts, bias_tables(): table[..., b][..., None]  16.4 us
    concatenate x1, other arithmetic, shards(): wide = jnp.concatenate([own, halo, fill], axis=2)  15.5 us
  transfers between devices with their start and end apart: 31, of which 1 were waited for; matrix products, arithmetic and copies ran while one was open for 49% of the time, Pallas kernels for 0%

profile of v1, /device:TPU:0, one launch (start us, length us, event | category | flops | bytes accessed | tf_op | source)
XLA Modules:
  0.0 511.9 jit_solution(10086685581605170165)
XLA Ops:
  11.8 5.9 %collective-permute-start.4 = (bf16[2,16,18,512]{3,1,2,0:T(8,128)(2,1)}, bf16[2,16,18,512]{3,1,2,0:T(8,128)(2,1)}, u32[]{:S(2)}, u32[]{:S(2)}) collective-permute-start(bf16[2,16,18,512]{3,1,2,0:T(8,128)(2,1)} %copy.50), channel_id=1, source_target_pairs={{0,2},{2,4},{4,6},{1,3},{3,5},{5,7},{8,10},{10,12},{12,14},{9,11},... | collective-permute-start | bytes 1769480 | tf_op jit(solution)/shard_map/ppermute | solution.py:23
  40.4 6.8 %broadcast_in_dim.305 = f32[6,128,1040]{2,1,0:T(8,128)} reshape(f32[6,4,32,13,80]{4,3,2,1,0:T(8,128)} %broadcast_in_dim.304) | data formatting | bytes 6389760 | tf_op jit(solution)/shard_map/jit(_where)/broadcast_in_dim | solution.py:127
  51.5 6.8 %broadcast_in_dim.311 = f32[6,128,1040]{2,1,0:T(8,128)} reshape(f32[6,4,32,13,80]{4,3,2,1,0:T(8,128)} %broadcast_in_dim.310) | data formatting | bytes 6389760 | tf_op jit(solution)/shard_map/jit(_where)/broadcast_in_dim | solution.py:127
  62.6 6.8 %broadcast_in_dim.317 = f32[6,128,1040]{2,1,0:T(8,128)} reshape(f32[6,4,32,13,80]{4,3,2,1,0:T(8,128)} %broadcast_in_dim.316) | data formatting | bytes 6389760 | tf_op jit(solution)/shard_map/jit(_where)/broadcast_in_dim | solution.py:127
  73.6 6.8 %broadcast_in_dim.323 = f32[6,128,1040]{2,1,0:T(8,128)} reshape(f32[6,4,32,13,80]{4,3,2,1,0:T(8,128)} %broadcast_in_dim.322) | data formatting | bytes 6389760 | tf_op jit(solution)/shard_map/jit(_where)/broadcast_in_dim | solution.py:127
  84.6 6.8 %broadcast_in_dim.329 = f32[6,128,1040]{2,1,0:T(8,128)} reshape(f32[6,4,32,13,80]{4,3,2,1,0:T(8,128)} %broadcast_in_dim.328) | data formatting | bytes 6389760 | tf_op jit(solution)/shard_map/jit(_where)/broadcast_in_dim | solution.py:127
  95.7 6.8 %broadcast_in_dim.335 = f32[6,128,1040]{2,1,0:T(8,128)} reshape(f32[6,4,32,13,80]{4,3,2,1,0:T(8,128)} %broadcast_in_dim.334) | data formatting | bytes 6389760 | tf_op jit(solution)/shard_map/jit(_where)/broadcast_in_dim | solution.py:127
  106.8 6.8 %broadcast_in_dim.341 = f32[6,128,1040]{2,1,0:T(8,128)} reshape(f32[6,4,32,13,80]{4,3,2,1,0:T(8,128)} %broadcast_in_dim.340) | data formatting | bytes 6389760 | tf_op jit(solution)/shard_map/jit(_where)/broadcast_in_dim | solution.py:127
  117.8 7.1 %broadcast_in_dim.347 = f32[6,128,1040]{2,1,0:T(8,128)} reshape(f32[6,4,32,13,80]{4,3,2,1,0:T(8,128)} %broadcast_in_dim.346) | data formatting | bytes 6389760 | tf_op jit(solution)/shard_map/jit(_where)/broadcast_in_dim | solution.py:127
  129.2 6.8 %broadcast_in_dim.353 = f32[6,128,1040]{2,1,0:T(8,128)} reshape(f32[6,4,32,13,80]{4,3,2,1,0:T(8,128)} %broadcast_in_dim.352) | data formatting | bytes 6389760 | tf_op jit(solution)/shard_map/jit(_where)/broadcast_in_dim | solution.py:127
  140.3 6.8 %broadcast_in_dim.359 = f32[6,128,1040]{2,1,0:T(8,128)} reshape(f32[6,4,32,13,80]{4,3,2,1,0:T(8,128)} %broadcast_in_dim.358) | data formatting | bytes 6389760 | tf_op jit(solution)/shard_map/jit(_where)/broadcast_in_dim | solution.py:127
  151.3 6.8 %broadcast_in_dim.365 = f32[6,128,1040]{2,1,0:T(8,128)} reshape(f32[6,4,32,13,80]{4,3,2,1,0:T(8,128)} %broadcast_in_dim.364) | data formatting | bytes 6389760 | tf_op jit(solution)/shard_map/jit(_where)/broadcast_in_dim | solution.py:127
  162.4 6.8 %broadcast_in_dim.371 = f32[6,128,1040]{2,1,0:T(8,128)} reshape(f32[6,4,32,13,80]{4,3,2,1,0:T(8,128)} %broadcast_in_dim.370) | data formatting | bytes 6389760 | tf_op jit(solution)/shard_map/jit(_where)/broadcast_in_dim | solution.py:127
  225.1 17.9 %select_select_fusion.bias_ref = f32[6,128,1040]{2,1,0:T(8,128)} fusion(f32[6,128,1040]{2,1,0:T(8,128)S(1)} %broadcast_in_dim.299, f32[6,128,1040]{2,1,0:T(8,128)} %broadcast_in_dim.305, f32[6,128,1040]{2,1,0:T(8,128)} %broadcast_in_dim.311, f32[6,128,1040]{2,1,0:T(8,128)} %broadcast_in_dim.317, f32[6,128,1040]{2,1,0:T(8,128)} %broadcast_in_dim.323, ...), kind=kLoop, calls=%fused_computation.13 | loop fusion | flops 10383360 | bytes 46458880 | tf_op jit(solution)/shard_map/jit(_where)/select_n | solution.py:127
  250.9 6.9 %collective-permute-start.20 = (bf16[2,16,32,512]{3,2,1,0:T(8,128)(2,1)}, bf16[2,16,32,512]{3,2,1,0:T(8,128)(2,1)}, u32[]{:S(2)}, u32[]{:S(2)}) collective-permute-start(bf16[2,16,32,512]{3,2,1,0:T(8,128)(2,1)} %pad_maximum_fusion.3), channel_id=1, source_target_pairs={{0,8},{8,16},{16,24},{1,9},{9,17},{17,25},{2,10},{10,18},{18,26},{... | collective-permute-start | bytes 3145736 | tf_op jit(solution)/shard_map/ppermute | solution.py:23
  291.3 9.0 %collective-permute-start.21 = (bf16[2,2,32,512]{3,2,1,0:T(8,128)(2,1)S(1)}, bf16[2,2,32,512]{3,2,1,0:T(8,128)(2,1)S(1)}, u32[]{:S(2)}, u32[]{:S(2)}) collective-permute-start(bf16[2,2,32,512]{3,2,1,0:T(8,128)(2,1)S(1)} %slice.217), channel_id=1, source_target_pairs={{0,8},{8,16},{16,24},{1,9},{9,17},{17,25},{2,10},{10,18},{18,26},{... | collective-permute-start | bytes 393224 | tf_op jit(solution)/shard_map/ppermute | solution.py:23
  329.9 9.6 %collective-permute-start.27 = (bf16[2,2,36,512]{3,2,1,0:T(8,128)(2,1)S(1)}, bf16[2,2,36,512]{3,2,1,0:T(8,128)(2,1)S(1)}, u32[]{:S(2)}, u32[]{:S(2)}) collective-permute-start(bf16[2,2,36,512]{3,2,1,0:T(8,128)(2,1)S(1)} %copy.102), channel_id=1, source_target_pairs={{0,8},{8,16},{16,24},{1,9},{9,17},{17,25},{2,10},{10,18},{18,26},{... | collective-permute-start | bytes 442376 | tf_op jit(solution)/shard_map/ppermute | solution.py:23
  352.8 15.5 %maximum_maximum_fusion = (bf16[2,52,80,512]{3,2,1,0:T(8,128)(2,1)}, bf16[2,52,80,512]{3,2,1,0:T(8,128)(2,1)S(1)}, bf16[2,52,80,512]{3,2,1,0:T(8,128)(2,1)}) fusion(bf16[2,52,36,512]{3,2,1,0:T(8,128)(2,1)S(1)} %constant_dynamic-update-slice_fusion.5, bf16[2,52,32,512]{3,2,1,0:T(8,128)(2,1)} %copy-done.18, bf16[80]{0:T(256)(128)(2,1)S(1)} %pad.27.clone, ...), kind=kLoop, calls=%fused_computation | loop fusion | flops 68157440 | bytes 47284384 | tf_op jit(solution)/shard_map/concatenate | solution.py:157
  378.2 25.9 %shard_map.84 = bf16[16,32,512]{2,1,0:T(8,128)(2,1)S(1)} custom-call(s32[1]{0:T(128)} %bitcast.54.dilation_ref, bf16[16,32,512]{2,1,0:T(8,128)(2,1)S(1)} %get-tuple-element.18.q_ref, bf16[52,80,512]{2,1,0:T(8,128)(2,1)S(1)} %get-tuple-element.10.k_ref, bf16[52,80,512]{2,1,0:T(8,128)(2,1)S(1)} %get-tuple-element.9.v_ref, f32[6,128,1040]{2,1,0:T(8,128)S(1)} %copy-done.2, ...), custom_call_target="tpu_custom_call" | custom-call | flops 17448304640 | bytes 8519680 | tf_op jit(solution)/shard_map/pallas_call | solution.py:82
  410.5 25.9 %shard_map.83 = bf16[16,32,512]{2,1,0:T(8,128)(2,1)S(1)} custom-call(s32[1]{0:T(128)} %bitcast.53.dilation_ref, bf16[16,32,512]{2,1,0:T(8,128)(2,1)S(1)} %get-tuple-element.19.q_ref, bf16[52,80,512]{2,1,0:T(8,128)(2,1)S(1)} %copy-done.1, bf16[52,80,512]{2,1,0:T(8,128)(2,1)S(1)} %copy-done, f32[6,128,1040]{2,1,0:T(8,128)S(1)} %copy-done.3, ...), custom_call_target="tpu_custom_call" | custom-call | flops 17448304640 | bytes 8519680 | tf_op jit(solution)/shard_map/pallas_call | solution.py:82
  436.4 25.9 %shard_map.82 = bf16[16,32,512]{2,1,0:T(8,128)(2,1)S(1)} custom-call(s32[1]{0:T(128)} %bitcast.52.dilation_ref, bf16[16,32,512]{2,1,0:T(8,128)(2,1)S(1)} %get-tuple-element.17.q_ref, bf16[52,80,512]{2,1,0:T(8,128)(2,1)S(1)} %get-tuple-element.6.k_ref, bf16[52,80,512]{2,1,0:T(8,128)(2,1)S(1)} %get-tuple-element.5.v_ref, f32[6,128,1040]{2,1,0:T(8,128)S(1)} %copy-done.3, ...), custom_call_target="tpu_custom_call" | custom-call | flops 17448304640 | bytes 8519680 | tf_op jit(solution)/shard_map/pallas_call | solution.py:82
  462.4 5.5 %fusion.4 = bf16[512,1536]{1,0:T(8,128)(2,1)S(1)} fusion(bf16[512,1536]{1,0:T(8,128)(2,1)S(1)} %bitcast.71, bf16[1536,3072]{1,0:T(8,128)(2,1)} %param.15, s32[]{:T(128)S(6)} %select_n.162), kind=kOutput, calls=%fused_computation.15 | convolution fusion | flops 2416705536 | bytes 7864324 | tf_op jit(solution)/shard_map/dot_general | solution.py:175
  469.5 35.6 %collective-permute-done.30 = bf16[512,1536]{1,0:T(8,128)(2,1)S(1)} collective-permute-done((bf16[512,1536]{1,0:T(8,128)(2,1)S(1)}, bf16[512,1536]{1,0:T(8,128)(2,1)S(1)}, u32[]{:S(2)}, u32[]{:S(2)}) %collective-permute-start.30) | collective-permute-done | bytes 1572896 | tf_op jit(solution)/shard_map/ppermute | solution.py:176
  505.1 6.6 %add_convert_fusion = bf16[512,1536]{1,0:T(8,128)(2,1)} fusion(bf16[512,1536]{1,0:T(8,128)(2,1)S(1)} %collective-permute-done.30, bf16[512,1536]{1,0:T(8,128)(2,1)} %bitcast.72, bf16[1536,3072]{1,0:T(8,128)(2,1)} %param.15, s32[]{:T(128)S(6)} %select_n.161), kind=kOutput, calls=%fused_computation.14 | convolution fusion | flops 2418278400 | bytes 9437188 | tf_op jit(solution)/shard_map/dot_general | solution.py:177
  (259 shorter events, 237.3 us)
Async XLA Ops:
  3.4 254.4 %collective-permute-start = (bf16[2,16,32,512]{3,2,1,0:T(8,128)(2,1)}, bf16[2,16,32,512]{3,2,1,0:T(8,128)(2,1)}, u32[]{:S(2)}, u32[]{:S(2)}) collective-permute-start(bf16[2,16,32,512]{3,2,1,0:T(8,128)(2,1)} %pad_maximum_fusion.1), channel_id=1, source_target_pairs={{0,8},{8,16},{16,24},{1,9},{9,17},{17,25},{2,10},{10,18},{18,26},{... | collective-permute-start | bytes 3145736 | tf_op jit(solution)/shard_map/ppermute | solution.py:23
  6.9 256.4 %collective-permute-start.2 = (bf16[2,16,32,512]{3,2,1,0:T(8,128)(2,1)}, bf16[2,16,32,512]{3,2,1,0:T(8,128)(2,1)}, u32[]{:S(2)}, u32[]{:S(2)}) collective-permute-start(bf16[2,16,32,512]{3,2,1,0:T(8,128)(2,1)} %pad_maximum_fusion.1), channel_id=1, source_target_pairs={{8,0},{16,8},{24,16},{9,1},{17,9},{25,17},{10,2},{18,10},{26,18},{... | collective-permute-start | bytes 3145736 | tf_op jit(solution)/shard_map/ppermute | solution.py:23
  9.4 203.6 %collective-permute-start.5 = (bf16[2,16,18,512]{3,1,2,0:T(8,128)(2,1)}, bf16[2,16,18,512]{3,1,2,0:T(8,128)(2,1)}, u32[]{:S(2)}, u32[]{:S(2)}) collective-permute-start(bf16[2,16,18,512]{3,1,2,0:T(8,128)(2,1)} %copy.51), channel_id=1, source_target_pairs={{2,0},{4,2},{6,4},{3,1},{5,3},{7,5},{10,8},{12,10},{14,12},{11,9},... | collective-permute-start | bytes 1769480 | tf_op jit(solution)/shard_map/ppermute | solution.py:23
  11.8 206.6 %collective-permute-start.4 = (bf16[2,16,18,512]{3,1,2,0:T(8,128)(2,1)}, bf16[2,16,18,512]{3,1,2,0:T(8,128)(2,1)}, u32[]{:S(2)}, u32[]{:S(2)}) collective-permute-start(bf16[2,16,18,512]{3,1,2,0:T(8,128)(2,1)} %copy.50), channel_id=1, source_target_pairs={{0,2},{2,4},{4,6},{1,3},{3,5},{5,7},{8,10},{10,12},{12,14},{9,11},... | collective-permute-start | bytes 1769480 | tf_op jit(solution)/shard_map/ppermute | solution.py:23
  19.2 200.4 %collective-permute-start.15 = (bf16[2,16,18,512]{3,1,2,0:T(8,128)(2,1)}, bf16[2,16,18,512]{3,1,2,0:T(8,128)(2,1)}, u32[]{:S(2)}, u32[]{:S(2)}) collective-permute-start(bf16[2,16,18,512]{3,1,2,0:T(8,128)(2,1)} %copy.75), channel_id=1, source_target_pairs={{2,0},{4,2},{6,4},{3,1},{5,3},{7,5},{10,8},{12,10},{14,12},{11,9},... | collective-permute-start | bytes 1769480 | tf_op jit(solution)/shard_map/ppermute | solution.py:23
  213.0 32.3 %collective-permute-start.14 = (bf16[2,16,18,512]{3,1,2,0:T(8,128)(2,1)}, bf16[2,16,18,512]{3,1,2,0:T(8,128)(2,1)}, u32[]{:S(2)}, u32[]{:S(2)}) collective-permute-start(bf16[2,16,18,512]{3,1,2,0:T(8,128)(2,1)} %copy.74), channel_id=1, source_target_pairs={{0,2},{2,4},{4,6},{1,3},{3,5},{5,7},{8,10},{10,12},{12,14},{9,11},... | collective-permute-start | bytes 1769480 | tf_op jit(solution)/shard_map/ppermute | solution.py:23
  218.4 31.3 %collective-permute-start.25 = (bf16[2,16,18,512]{3,1,2,0:T(8,128)(2,1)}, bf16[2,16,18,512]{3,1,2,0:T(8,128)(2,1)}, u32[]{:S(2)}, u32[]{:S(2)}) collective-permute-start(bf16[2,16,18,512]{3,1,2,0:T(8,128)(2,1)} %copy.85), channel_id=1, source_target_pairs={{2,0},{4,2},{6,4},{3,1},{5,3},{7,5},{10,8},{12,10},{14,12},{11,9},... | collective-permute-start | bytes 1769480 | tf_op jit(solution)/shard_map/ppermute | solution.py:23
  219.7 31.3 %collective-permute-start.24 = (bf16[2,16,18,512]{3,1,2,0:T(8,128)(2,1)}, bf16[2,16,18,512]{3,1,2,0:T(8,128)(2,1)}, u32[]{:S(2)}, u32[]{:S(2)}) collective-permute-start(bf16[2,16,18,512]{3,1,2,0:T(8,128)(2,1)} %copy.84), channel_id=1, source_target_pairs={{0,2},{2,4},{4,6},{1,3},{3,5},{5,7},{8,10},{10,12},{12,14},{9,11},... | collective-permute-start | bytes 1769480 | tf_op jit(solution)/shard_map/ppermute | solution.py:23
  245.3 28.9 %collective-permute-start.10 = (bf16[2,16,32,512]{3,2,1,0:T(8,128)(2,1)}, bf16[2,16,32,512]{3,2,1,0:T(8,128)(2,1)S(1)}, u32[]{:S(2)}, u32[]{:S(2)}) collective-permute-start(bf16[2,16,32,512]{3,2,1,0:T(8,128)(2,1)} %pad_maximum_fusion.2), channel_id=1, source_target_pairs={{0,8},{8,16},{16,24},{1,9},{9,17},{17,25},{2,10},{10,18},{18,26},{... | collective-permute-start | bytes 3145736 | tf_op jit(solution)/shard_map/ppermute | solution.py:23
  249.6 29.8 %collective-permute-start.12 = (bf16[2,16,32,512]{3,2,1,0:T(8,128)(2,1)}, bf16[2,16,32,512]{3,2,1,0:T(8,128)(2,1)}, u32[]{:S(2)}, u32[]{:S(2)}) collective-permute-start(bf16[2,16,32,512]{3,2,1,0:T(8,128)(2,1)} %pad_maximum_fusion.2), channel_id=1, source_target_pairs={{8,0},{16,8},{24,16},{9,1},{17,9},{25,17},{10,2},{18,10},{26,18},{... | collective-permute-start | bytes 3145736 | tf_op jit(solution)/shard_map/ppermute | solution.py:23
  250.9 30.8 %collective-permute-start.20 = (bf16[2,16,32,512]{3,2,1,0:T(8,128)(2,1)}, bf16[2,16,32,512]{3,2,1,0:T(8,128)(2,1)}, u32[]{:S(2)}, u32[]{:S(2)}) collective-permute-start(bf16[2,16,32,512]{3,2,1,0:T(8,128)(2,1)} %pad_maximum_fusion.3), channel_id=1, source_target_pairs={{0,8},{8,16},{16,24},{1,9},{9,17},{17,25},{2,10},{10,18},{18,26},{... | collective-permute-start | bytes 3145736 | tf_op jit(solution)/shard_map/ppermute | solution.py:23
  257.8 26.1 %collective-permute-start.22 = (bf16[2,16,32,512]{3,2,1,0:T(8,128)(2,1)}, bf16[2,16,32,512]{3,2,1,0:T(8,128)(2,1)}, u32[]{:S(2)}, u32[]{:S(2)}) collective-permute-start(bf16[2,16,32,512]{3,2,1,0:T(8,128)(2,1)} %pad_maximum_fusion.3), channel_id=1, source_target_pairs={{8,0},{16,8},{24,16},{9,1},{17,9},{25,17},{10,2},{18,10},{26,18},{... | collective-permute-start | bytes 3145736 | tf_op jit(solution)/shard_map/ppermute | solution.py:23
  263.3 48.1 %collective-permute-start.6 = (bf16[2,16,36,512]{3,1,2,0:T(8,128)(2,1)S(1)}, bf16[2,16,36,512]{3,1,2,0:T(8,128)(2,1)S(1)}, u32[]{:S(2)}, u32[]{:S(2)}) collective-permute-start(bf16[2,16,36,512]{3,1,2,0:T(8,128)(2,1)S(1)} %copy.54), channel_id=1, source_target_pairs={{0,8},{8,16},{16,24},{1,9},{9,17},{17,25},{2,10},{10,18},{18,26},{... | collective-permute-start | bytes 3538952 | tf_op jit(solution)/shard_map/ppermute | solution.py:23
  279.5 38.6 %collective-permute-start.8 = (bf16[2,16,36,512]{3,1,2,0:T(8,128)(2,1)S(1)}, bf16[2,16,36,512]{3,1,2,0:T(8,128)(2,1)S(1)}, u32[]{:S(2)}, u32[]{:S(2)}) collective-permute-start(bf16[2,16,36,512]{3,1,2,0:T(8,128)(2,1)S(1)} %copy.54), channel_id=1, source_target_pairs={{8,0},{16,8},{24,16},{9,1},{17,9},{25,17},{10,2},{18,10},{26,18},{... | collective-permute-start | bytes 3538952 | tf_op jit(solution)/shard_map/ppermute | solution.py:23
  284.0 16.4 %collective-permute-start.11 = (bf16[2,2,32,512]{3,2,1,0:T(8,128)(2,1)S(1)}, bf16[2,2,32,512]{3,2,1,0:T(8,128)(2,1)S(1)}, u32[]{:S(2)}, u32[]{:S(2)}) collective-permute-start(bf16[2,2,32,512]{3,2,1,0:T(8,128)(2,1)S(1)} %slice.207), channel_id=1, source_target_pairs={{0,8},{8,16},{16,24},{1,9},{9,17},{17,25},{2,10},{10,18},{18,26},{... | collective-permute-start | bytes 393224 | tf_op jit(solution)/shard_map/ppermute | solution.py:23
  303.0 19.4 %collective-permute-start.16 = (bf16[2,16,36,512]{3,1,2,0:T(8,128)(2,1)S(1)}, bf16[2,16,36,512]{3,1,2,0:T(8,128)(2,1)S(1)}, u32[]{:S(2)}, u32[]{:S(2)}) collective-permute-start(bf16[2,16,36,512]{3,1,2,0:T(8,128)(2,1)S(1)} %copy.78), channel_id=1, source_target_pairs={{0,8},{8,16},{16,24},{1,9},{9,17},{17,25},{2,10},{10,18},{18,26},{... | collective-permute-start | bytes 3538952 | tf_op jit(solution)/shard_map/ppermute | solution.py:23
  306.3 17.7 %collective-permute-start.18 = (bf16[2,16,36,512]{3,1,2,0:T(8,128)(2,1)S(1)}, bf16[2,16,36,512]{3,1,2,0:T(8,128)(2,1)S(1)}, u32[]{:S(2)}, u32[]{:S(2)}) collective-permute-start(bf16[2,16,36,512]{3,1,2,0:T(8,128)(2,1)S(1)} %copy.78), channel_id=1, source_target_pairs={{8,0},{16,8},{24,16},{9,1},{17,9},{25,17},{10,2},{18,10},{26,18},{... | collective-permute-start | bytes 3538952 | tf_op jit(solution)/shard_map/ppermute | solution.py:23
  307.6 20.8 %collective-permute-start.26 = (bf16[2,16,36,512]{3,1,2,0:T(8,128)(2,1)S(1)}, bf16[2,16,36,512]{3,1,2,0:T(8,128)(2,1)S(1)}, u32[]{:S(2)}, u32[]{:S(2)}) collective-permute-start(bf16[2,16,36,512]{3,1,2,0:T(8,128)(2,1)S(1)} %copy.88), channel_id=1, source_target_pairs={{0,8},{8,16},{16,24},{1,9},{9,17},{17,25},{2,10},{10,18},{18,26},{... | collective-permute-start | bytes 3538952 | tf_op jit(solution)/shard_map/ppermute | solution.py:23
  311.4 18.5 %collective-permute-start.28 = (bf16[2,16,36,512]{3,1,2,0:T(8,128)(2,1)S(1)}, bf16[2,16,36,512]{3,1,2,0:T(8,128)(2,1)S(1)}, u32[]{:S(2)}, u32[]{:S(2)}) collective-permute-start(bf16[2,16,36,512]{3,1,2,0:T(8,128)(2,1)S(1)} %copy.88), channel_id=1, source_target_pairs={{8,0},{16,8},{24,16},{9,1},{17,9},{25,17},{10,2},{18,10},{26,18},{... | collective-permute-start | bytes 3538952 | tf_op jit(solution)/shard_map/ppermute | solution.py:23
  318.1 21.6 %collective-permute-start.7 = (bf16[2,2,36,512]{3,2,1,0:T(8,128)(2,1)S(1)}, bf16[2,2,36,512]{3,2,1,0:T(8,128)(2,1)S(1)}, u32[]{:S(2)}, u32[]{:S(2)}) collective-permute-start(bf16[2,2,36,512]{3,2,1,0:T(8,128)(2,1)S(1)} %copy.106), channel_id=1, source_target_pairs={{0,8},{8,16},{16,24},{1,9},{9,17},{17,25},{2,10},{10,18},{18,26},{... | collective-permute-start | bytes 442376 | tf_op jit(solution)/shard_map/ppermute | solution.py:23
  322.5 27.5 %collective-permute-start.9 = (bf16[2,2,36,512]{3,2,1,0:T(8,128)(2,1)S(1)}, bf16[2,2,36,512]{3,2,1,0:T(8,128)(2,1)S(1)}, u32[]{:S(2)}, u32[]{:S(2)}) collective-permute-start(bf16[2,2,36,512]{3,2,1,0:T(8,128)(2,1)S(1)} %copy.107), channel_id=1, source_target_pairs={{8,0},{16,8},{24,16},{9,1},{17,9},{25,17},{10,2},{18,10},{26,18},{... | collective-permute-start | bytes 442376 | tf_op jit(solution)/shard_map/ppermute | solution.py:23
  324.0 17.7 %collective-permute-start.17 = (bf16[2,2,36,512]{3,2,1,0:T(8,128)(2,1)S(1)}, bf16[2,2,36,512]{3,2,1,0:T(8,128)(2,1)S(1)}, u32[]{:S(2)}, u32[]{:S(2)}) collective-permute-start(bf16[2,2,36,512]{3,2,1,0:T(8,128)(2,1)S(1)} %copy.104), channel_id=1, source_target_pairs={{0,8},{8,16},{16,24},{1,9},{9,17},{17,25},{2,10},{10,18},{18,26},{... | collective-permute-start | bytes 442376 | tf_op jit(solution)/shard_map/ppermute | solution.py:23
  328.4 21.6 %collective-permute-start.19 = (bf16[2,2,36,512]{3,2,1,0:T(8,128)(2,1)S(1)}, bf16[2,2,36,512]{3,2,1,0:T(8,128)(2,1)S(1)}, u32[]{:S(2)}, u32[]{:S(2)}) collective-permute-start(bf16[2,2,36,512]{3,2,1,0:T(8,128)(2,1)S(1)} %copy.105), channel_id=1, source_target_pairs={{8,0},{16,8},{24,16},{9,1},{17,9},{25,17},{10,2},{18,10},{26,18},{... | collective-permute-start | bytes 442376 | tf_op jit(solution)/shard_map/ppermute | solution.py:23
  467.9 37.2 %collective-permute-start.30 = (bf16[512,1536]{1,0:T(8,128)(2,1)S(1)}, bf16[512,1536]{1,0:T(8,128)(2,1)S(1)}, u32[]{:S(2)}, u32[]{:S(2)}) collective-permute-start(bf16[512,1536]{1,0:T(8,128)(2,1)S(1)} %fusion.4), channel_id=1, source_target_pairs={{0,1},{1,0},{2,3},{3,2},{4,5},{5,4},{6,7},{7,6},{8,9},{9,8},{10,11... | collective-permute-start | bytes 4718600 | tf_op jit(solution)/shard_map/ppermute | solution.py:176
  (34 other events, 340.1 us)

commit v2 on v1

v2 whole, which is shorter than its diff:
```python
import functools
import math

import jax
import jax.numpy as jnp
from jax import lax
from jax.experimental import pallas as pl
from jax.experimental.pallas import tpu as pltpu
from jax.sharding import PartitionSpec as P

HEAD_DIM = 64
RADIUS_MAX = 6
WINDOW = 13
HALO = 18
GROUP = 4
GROUP_FEATURES = GROUP * HEAD_DIM
MASKED = -1e30


def shifted(value, axis, steps):
    count = lax.axis_size(axis)
    first, last = (max(0, -steps), min(count, count - steps))
    return lax.ppermute(value, axis, [(source, source + steps) for source in range(first, last)])


def attention_kernel(
    rows, first_row, dilation_ref, q_ref, *refs
):
    pieces, (spot_ref, table_ref, row_ref, out_ref, kv_ref, bias_ref) = refs[:5], refs[5:]
    dilation = dilation_ref[0]
    cols = q_ref.shape[1]
    lane_head = lax.broadcasted_iota(jnp.int32, (cols, GROUP_FEATURES), 1) // HEAD_DIM

    filled = pieces[0].shape[2]
    tail = filled // 16 * 16
    top = 0
    for piece in pieces:
        count = piece.shape[1]
        for which in range(2):
            kv_ref[which, top : top + count, tail:] = jnp.zeros(
                (count, kv_ref.shape[2] - tail, GROUP_FEATURES), jnp.bfloat16
            )
            kv_ref[which, top : top + count, :filled] = piece[which]
        top += count
    spot = spot_ref[...]
    for h in range(GROUP):
        table = jnp.full(spot.shape, MASKED, jnp.float32)
        for b in range(WINDOW):
            table = jnp.where(spot == b, table_ref[h, b : b + 1, :], table)
        bias_ref[h * cols : (h + 1) * cols] = table

    def one_row(i, carry):
        query = q_ref[i] * jnp.bfloat16(1.0 / math.sqrt(HEAD_DIM))
        zero = jnp.zeros_like(query)
        stacked = jnp.concatenate(
            [jnp.where(lane_head == h, query, zero) for h in range(GROUP)], axis=0
        )
        places = [i + first_row + HALO + (a - RADIUS_MAX) * dilation for a in range(WINDOW)]
        keys = jnp.concatenate([kv_ref[0, place] for place in places], axis=0)
        scores = lax.dot_general(
            stacked, keys, (((1,), (1,)), ((), ())), preferred_element_type=jnp.float32
        )
        scores = scores + bias_ref[...] + row_ref[pl.ds(i, 1), :]
        peak = jnp.max(scores, axis=1, keepdims=True)
        exponent = jnp.exp(scores - peak)
        total = jnp.sum(exponent, axis=1, keepdims=True)
        values = jnp.concatenate([kv_ref[1, place] for place in places], axis=0)
        summed = jnp.dot(
            exponent.astype(jnp.bfloat16), values, preferred_element_type=jnp.float32
        )
        summed = summed / total
        result = summed[:cols]
        for h in range(1, GROUP):
            result = jnp.where(lane_head == h, summed[h * cols : (h + 1) * cols], result)
        out_ref[i] = result.astype(jnp.bfloat16)
        return carry

    lax.fori_loop(0, rows, one_row, 0)


def attend(dilation, query, pieces, spot, table, row_bias, first_group, groups, part, parts):
    tile_rows, cols, _ = query.shape
    rows = tile_rows // parts
    depth = spot.shape[1]
    key_cols = depth // WINDOW
    span_rows = sum(piece.shape[1] for piece in pieces)
    stacked = GROUP * cols
    return pl.pallas_call(
        functools.partial(attention_kernel, rows, part * rows),
        grid=(groups,),
        in_specs=[
            pl.BlockSpec(memory_space=pltpu.SMEM),
            pl.BlockSpec((rows, cols, GROUP_FEATURES), lambda g: (part, 0, g + first_group)),
            *[
                pl.BlockSpec((*piece.shape[:3], GROUP_FEATURES), lambda g: (0, 0, 0, g))
                for piece in pieces
            ],
            pl.BlockSpec((cols, depth), lambda g: (0, 0)),
            pl.BlockSpec((GROUP, WINDOW, depth), lambda g: (g + first_group, 0, 0)),
            pl.BlockSpec((rows, depth), lambda g: (part, 0)),
        ],
        out_specs=pl.BlockSpec((rows, cols, GROUP_FEATURES), lambda g: (0, 0, g)),
        out_shape=jax.ShapeDtypeStruct((rows, cols, groups * GROUP_FEATURES), jnp.bfloat16),
        scratch_shapes=[
            pltpu.VMEM((2, span_rows, key_cols, GROUP_FEATURES), jnp.bfloat16),
            pltpu.VMEM((stacked, depth), jnp.float32),
        ],
        compiler_params=pltpu.CompilerParams(vmem_limit_bytes=40 * 1024 * 1024),
        cost_estimate=pl.CostEstimate(
            flops=groups * rows * 12 * stacked * depth * GROUP_FEATURES,
            bytes_accessed=sum(piece.size for piece in pieces) * 2,
            transcendentals=groups * rows * stacked * depth,
        ),
    )(dilation, query, *pieces, spot, table, row_bias)


def bias_parts(rel_bias, pattern, radius, dilation, tile_rows, tile_cols, key_cols):
    heads = rel_bias.shape[0]
    depth = WINDOW * key_cols
    total_rows = tile_rows * lax.axis_size("row")
    total_cols = tile_cols * lax.axis_size("col")
    row_anchor = lax.axis_index("row") * tile_rows
    col_anchor = lax.axis_index("col") * tile_cols
    steps = jnp.arange(WINDOW, dtype=jnp.int32) - RADIUS_MAX
    spot = lax.broadcasted_iota(jnp.int32, (tile_cols, depth), 1) % key_cols
    column = lax.broadcasted_iota(jnp.int32, (tile_cols, depth), 0)
    offset = jnp.where(
        spot < tile_cols, spot, jnp.where(spot < tile_cols + HALO, spot - tile_cols - HALO, spot - HALO)
    )
    real = spot < tile_cols + 2 * HALO
    global_col = col_anchor + offset
    inside = real & (global_col >= 0) & (global_col < total_cols)
    step_of = jnp.full((tile_cols, depth), -1, jnp.int32)
    for b in range(WINDOW):
        hit = (offset - column == (b - RADIUS_MAX) * dilation) & inside
        step_of = jnp.where(hit, b, step_of)
    chosen = (pattern == 1) | ((steps[:, None] == 0) & (steps[None, :] == 0))
    chosen = chosen & (jnp.abs(steps)[:, None] <= radius) & (jnp.abs(steps)[None, :] <= radius)
    table = jnp.where(chosen[None], rel_bias, MASKED).transpose(0, 2, 1)
    table = jnp.broadcast_to(table[..., None], (heads, WINDOW, WINDOW, key_cols))
    row_step = lax.broadcasted_iota(jnp.int32, (tile_rows, depth), 1) // key_cols - RADIUS_MAX
    row_global = (
        row_anchor + lax.broadcasted_iota(jnp.int32, (tile_rows, depth), 0) + row_step * dilation
    )
    row_fine = (row_global >= 0) & (row_global < total_rows)
    row_bias = jnp.where(row_fine, 0.0, MASKED).astype(jnp.float32)
    return step_of, table.reshape(heads, WINDOW, depth), row_bias


def shards(
    query_map, key_map, value_map, window_mask, tile_radius, dilation_per_tile, rel_bias, out_weight
):
    tile_rows, tile_cols, features = query_map.shape
    key_cols = -(-(tile_cols + 2 * HALO) // 16) * 16
    dilation = dilation_per_tile[0, 0]
    spot, table, row_bias = bias_parts(
        rel_bias, window_mask[0, 0], tile_radius[0, 0], dilation, tile_rows, tile_cols, key_cols
    )
    groups = features // GROUP_FEATURES
    chunks = 2 if groups % 2 == 0 else 1
    spill = HALO - tile_rows
    width = features // chunks
    per_chunk = groups // chunks
    parts = 2 if tile_rows % 16 == 0 else 1
    tokens = tile_rows * tile_cols // parts
    blocks = [[] for _ in range(parts)]
    for c in range(chunks):
        cut = slice(c * width, (c + 1) * width)
        pair = jnp.stack([key_map[..., cut], value_map[..., cut]])
        left = shifted(pair[:, :, tile_cols - HALO :], "col", 1)
        right = shifted(pair[:, :, :HALO], "col", -1)
        wide = jnp.concatenate([pair, left, right], axis=2)
        pieces = [
            shifted(wide[:, tile_rows - spill :], "row", 2),
            shifted(wide, "row", 1),
            wide,
            shifted(wide, "row", -1),
            shifted(wide[:, :spill], "row", -2),
        ]
        split = parts if c == chunks - 1 else 1
        outs = [
            attend(
                dilation.reshape(1), query_map, pieces, spot, table, row_bias,
                c * per_chunk, per_chunk, part, split,
            ).reshape(-1, width)
            for part in range(split)
        ]
        for part in range(parts):
            if split == parts:
                blocks[part].append(outs[part])
            else:
                blocks[part].append(outs[0][part * tokens : (part + 1) * tokens])
    attended = [jnp.concatenate(block, axis=1) for block in blocks]
    count = lax.axis_size("head")
    model = out_weight.shape[1]
    if count != 2:
        partials = jnp.dot(
            jnp.concatenate(attended), out_weight, preferred_element_type=jnp.float32
        )
        mixed = lax.psum_scatter(partials, "head", scatter_dimension=1, tiled=True)
        return mixed.astype(jnp.bfloat16).reshape(tile_rows, tile_cols, model // count)
    me = lax.axis_index("head")
    half = model // 2
    theirs = lax.dynamic_slice_in_dim(out_weight, (1 - me) * half, half, 1)
    mine = lax.dynamic_slice_in_dim(out_weight, me * half, half, 1)
    mixed = []
    for block in attended:
        sent = jnp.dot(block, theirs, preferred_element_type=jnp.float32).astype(jnp.bfloat16)
        got = lax.ppermute(sent, "head", [(0, 1), (1, 0)])
        kept = jnp.dot(block, mine, preferred_element_type=jnp.float32)
        mixed.append((kept + got.astype(jnp.float32)).astype(jnp.bfloat16))
    return jnp.concatenate(mixed).reshape(tile_rows, tile_cols, half)


def solution(mesh):
    placed = (
        P("row", "col", "head"),
        P("row", "col", "head"),
        P("row", "col", "head"),
        P("row", "col", None, None),
        P("row", "col"),
        P("row", "col"),
        P("head", None, None),
        P("head", None),
    )
    return jax.shard_map(
        shards, mesh=mesh, in_specs=placed, out_specs=P("row", "col", "head"), check_vma=False
    )
```

time: 519 us -> 252 us (0.49); the launches traced: 512 us -> 250 us
  local copies, waits for them, and re-layouts: 244 us -> 42.2 us
  starting transfers between devices: 94.8 us -> 39.1 us
  other arithmetic: 44.7 us -> 6.83 us
  waiting for transfers between devices: 35.7 us -> 60.3 us
  Pallas kernels: 77.6 us -> 88.9 us
    broadcast_in_dim x53 -> x1, local copies, waits for them, and re-layouts: 171 us -> 2.8 us  [bias_parts(): jnp.broadcast_to(table[..., None], (heads, WINDOW, WINDOW, key_cols))]
    ppermute x30 -> x12, starting transfers between devices: 93.2 us -> 37 us  [shifted(): lax.ppermute(value, axis, [(source, source + steps) for source in range(f...]
    ppermute x30 -> x12, waiting for transfers between devices: 0.08 us -> 50.5 us  [shifted(): lax.ppermute(value, axis, [(source, source + steps) for source in range(f...]
    ppermute x1 -> x2, waiting for transfers between devices: 35.6 us -> 9.83 us  [shards(): got = lax.ppermute(sent, 'head', [(0, 1), (1, 0)])]
    unnamed x78 -> x30, local copies, waits for them, and re-layouts: 24.7 us -> 0.09 us
    slice x33 -> x7, local copies, waits for them, and re-layouts: 27.9 us -> 4.69 us  [the longest x2 2.19 us: shards(): wide[:, :spill]]
    select_n x4 -> x2, other arithmetic: 18.1 us -> 1.69 us  [the longest x1 0.99 us: bias_parts(): step_of = jnp.where(hit, b, step_of)]
    concatenate x5 -> x3, other arithmetic: 16.7 us -> 3.21 us  [the longest x2 1.96 us: shards(): wide = jnp.concatenate([pair, left, right], axis=2)]
  transfers between devices with their start and end apart: 31 -> 14, of which waited for: 1 -> 6; matrix products, arithmetic and copies ran while one was open for 49% -> 19% of each run, Pallas kernels for 0% -> 26%
where the time goes in v2:
time: 252 us; the launch traced here: 250 us
  Pallas kernels  88.9 us (35%)
  waiting for transfers between devices  60.3 us (24%)
  local copies, waits for them, and re-layouts  42.2 us (17%)
  starting transfers between devices  39.1 us (16%)
  matrix products  11.3 us (4%)
  other arithmetic  6.83 us (3%)
    pallas_call x3, Pallas kernels, attend(): pl.pallas_call(functools.partial(attention_kernel, rows, part * rows), gr...  88.9 us
    ppermute x12, waiting for transfers between devices, shifted(): lax.ppermute(value, axis, [(source, source + steps) for source in range(f...  50.5 us
    ppermute x12, starting transfers between devices, shifted(): lax.ppermute(value, axis, [(source, source + steps) for source in range(f...  37 us
    ppermute x8, local copies, waits for them, and re-layouts, shifted(): lax.ppermute(value, axis, [(source, source + steps) for source in range(f...  19.5 us
    ppermute x2, waiting for transfers between devices, shards(): got = lax.ppermute(sent, 'head', [(0, 1), (1, 0)])  9.83 us
    dot_general x2, matrix products, shards(): kept = jnp.dot(block, mine, preferred_element_type=jnp.float32)  7.65 us
    reshape x2, local copies, waits for them, and re-layouts, bias_parts(): return (step_of, table.reshape(heads, WINDOW, depth), row_bias)  6.09 us
    concatenate x2, local copies, waits for them, and re-layouts, shards(): wide = jnp.concatenate([pair, left, right], axis=2)  5.24 us
  transfers between devices with their start and end apart: 14, of which 6 were waited for; matrix products, arithmetic and copies ran while one was open for 19% of the time, Pallas kernels for 26%

profile of v2, /device:TPU:0, one launch (start us, length us, event | category | flops | bytes accessed | tf_op | source)
XLA Modules:
  0.0 250.4 jit_solution(13801900371159752499)
XLA Ops:
  4.2 5.6 %collective-permute-start = (bf16[2,16,18,768]{3,1,2,0:T(8,128)(2,1)S(1)}, bf16[2,16,18,768]{3,1,2,0:T(8,128)(2,1)S(1)}, u32[]{:S(2)}, u32[]{:S(2)}) collective-permute-start(bf16[2,16,18,768]{3,1,2,0:T(8,128)(2,1)S(1)} %copy.14), channel_id=1, source_target_pairs={{0,2},{2,4},{4,6},{1,3},{3,5},{5,7},{8,10},{10,12},{12,14},{9,11},... | collective-permute-start | bytes 2654216 | tf_op jit(solution)/shard_map/ppermute | solution.py:23
  9.9 17.5 %collective-permute-done.1 = bf16[2,16,18,768]{3,1,2,0:T(8,128)(2,1)S(1)} collective-permute-done((bf16[2,16,18,768]{3,1,2,0:T(8,128)(2,1)S(1)}, bf16[2,16,18,768]{3,1,2,0:T(8,128)(2,1)S(1)}, u32[]{:S(2)}, u32[]{:S(2)}) %collective-permute-start.1) | collective-permute-done | bytes 884768 | tf_op jit(solution)/shard_map/ppermute | solution.py:23
  30.0 2.5 copy.18
  33.7 4.9 %collective-permute-start.3 = (bf16[2,16,68,768]{3,1,2,0:T(8,128)(2,1)}, bf16[2,16,68,768]{3,1,2,0:T(8,128)(2,1)}, u32[]{:S(2)}, u32[]{:S(2)}) collective-permute-start(bf16[2,16,68,768]{3,1,2,0:T(8,128)(2,1)} %copy.18), channel_id=1, source_target_pairs={{0,8},{8,16},{16,24},{1,9},{9,17},{17,25},{2,10},{10,18},{18,26},{... | collective-permute-start | bytes 10027016 | tf_op jit(solution)/shard_map/ppermute | solution.py:23
  42.6 5.9 %collective-permute-start.6 = (bf16[2,16,18,768]{3,1,2,0:T(8,128)(2,1)}, bf16[2,16,18,768]{3,1,2,0:T(8,128)(2,1)}, u32[]{:S(2)}, u32[]{:S(2)}) collective-permute-start(bf16[2,16,18,768]{3,1,2,0:T(8,128)(2,1)} %copy.24), channel_id=1, source_target_pairs={{0,2},{2,4},{4,6},{1,3},{3,5},{5,7},{8,10},{10,12},{12,14},{9,11},... | collective-permute-start | bytes 2654216 | tf_op jit(solution)/shard_map/ppermute | solution.py:23
  50.6 13.5 %collective-permute-done.7 = bf16[2,16,18,768]{3,1,2,0:T(8,128)(2,1)} collective-permute-done((bf16[2,16,18,768]{3,1,2,0:T(8,128)(2,1)}, bf16[2,16,18,768]{3,1,2,0:T(8,128)(2,1)}, u32[]{:S(2)}, u32[]{:S(2)}) %collective-permute-start.7) | collective-permute-done | bytes 884768 | tf_op jit(solution)/shard_map/ppermute | solution.py:23
  68.9 2.8 %copy.28 = bf16[2,16,68,768]{3,1,2,0:T(8,128)(2,1)} copy(bf16[2,16,68,768]{3,2,1,0:T(8,128)(2,1)S(1)} %pad_maximum_fusion.1.refs_2_) | data formatting | bytes 6684672 | tf_op jit(solution)/shard_map/concatenate | solution.py:172
  73.0 4.8 %collective-permute-start.9 = (bf16[2,16,68,768]{3,1,2,0:T(8,128)(2,1)}, bf16[2,16,68,768]{3,1,2,0:T(8,128)(2,1)}, u32[]{:S(2)}, u32[]{:S(2)}) collective-permute-start(bf16[2,16,68,768]{3,1,2,0:T(8,128)(2,1)} %copy.28), channel_id=1, source_target_pairs={{0,8},{8,16},{16,24},{1,9},{9,17},{17,25},{2,10},{10,18},{18,26},{... | collective-permute-start | bytes 10027016 | tf_op jit(solution)/shard_map/ppermute | solution.py:23
  81.1 6.1 %collective-permute-start.2 = (bf16[2,2,68,768]{3,2,1,0:T(8,128)(2,1)}, bf16[2,2,68,768]{3,2,1,0:T(8,128)(2,1)}, u32[]{:S(2)}, u32[]{:S(2)}) collective-permute-start(bf16[2,2,68,768]{3,2,1,0:T(8,128)(2,1)} %get-tuple-element.6), channel_id=1, source_target_pairs={{0,16},{8,24},{1,17},{9,25},{2,18},{10,26},{3,19},{11,27},{4,20},{... | collective-permute-start | bytes 1253384 | tf_op jit(solution)/shard_map/ppermute | solution.py:23
  89.7 2.8 %broadcast_in_dim.87 = f32[24,13,13,80]{3,2,0,1:T(8,128)} broadcast(f32[24,13,13]{2,0,1:T(8,128)} %copy.20), dimensions={0,1,2} | broadcast | bytes 1314144 | tf_op jit(solution)/shard_map/broadcast_in_dim | solution.py:140
  92.5 3.2 %reshape.101 = f32[24,13,1040]{2,0,1:T(8,128)} reshape(f32[24,13,13,80]{3,2,0,1:T(8,128)} %broadcast_in_dim.87) | data formatting | bytes 2595840 | tf_op jit(solution)/shard_map/reshape | solution.py:147
  95.7 2.9 %copy.23.refs_6_ = f32[24,13,1040]{2,1,0:T(8,128)} copy(f32[24,13,1040]{2,0,1:T(8,128)} %reshape.101) | data formatting | bytes 2595840 | tf_op jit(solution)/shard_map/reshape | solution.py:147
  99.8 4.9 %copy.22.refs_3_ = bf16[2,16,68,768]{3,2,1,0:T(8,128)(2,1)} copy(bf16[2,16,68,768]{3,1,2,0:T(8,128)(2,1)} %collective-permute-done.4) | data formatting | bytes 6684672 | tf_op jit(solution)/shard_map/ppermute | solution.py:23
  106.3 3.1 %copy.21.refs_1_ = bf16[2,16,68,768]{3,2,1,0:T(8,128)(2,1)S(1)} copy(bf16[2,16,68,768]{3,1,2,0:T(8,128)(2,1)} %collective-permute-done.3) | data formatting | bytes 6684672 | tf_op jit(solution)/shard_map/ppermute | solution.py:23
  109.3 17.5 %collective-permute-done.5.refs_4_ = bf16[2,2,68,768]{3,2,1,0:T(8,128)(2,1)} collective-permute-done((bf16[2,2,68,768]{3,2,1,0:T(8,128)(2,1)}, bf16[2,2,68,768]{3,2,1,0:T(8,128)(2,1)}, u32[]{:S(2)}, u32[]{:S(2)}) %collective-permute-start.5) | collective-permute-done | bytes 417824 | tf_op jit(solution)/shard_map/ppermute | solution.py:23
  128.6 42.2 %shard_map.82 = bf16[16,32,768]{2,1,0:T(8,128)(2,1)S(1)} custom-call(s32[1]{0:T(128)} %bitcast.27.dilation_ref, bf16[16,32,1536]{2,1,0:T(8,128)(2,1)S(1)} %copy-done.5, bf16[2,2,68,768]{3,2,1,0:T(8,128)(2,1)} %collective-permute-done.2.refs_0_, bf16[2,16,68,768]{3,2,1,0:T(8,128)(2,1)S(1)} %copy.21.refs_1_, ...), custom_call_target="tpu_custom_call" | custom-call | flops 19629342720 | bytes 10862592 | tf_op jit(solution)/shard_map/pallas_call | solution.py:88
  170.8 4.9 %copy.31.refs_3_ = bf16[2,16,68,768]{3,2,1,0:T(8,128)(2,1)} copy(bf16[2,16,68,768]{3,1,2,0:T(8,128)(2,1)} %collective-permute-done.10) | data formatting | bytes 6684672 | tf_op jit(solution)/shard_map/ppermute | solution.py:23
  175.7 3.2 %copy.30.refs_1_ = bf16[2,16,68,768]{3,2,1,0:T(8,128)(2,1)S(1)} copy(bf16[2,16,68,768]{3,1,2,0:T(8,128)(2,1)} %collective-permute-done.9) | data formatting | bytes 6684672 | tf_op jit(solution)/shard_map/ppermute | solution.py:23
  179.0 23.4 %shard_map.83 = bf16[8,32,768]{2,1,0:T(8,128)(2,1)S(1)} custom-call(s32[1]{0:T(128)} %bitcast.28.dilation_ref, bf16[16,32,1536]{2,1,0:T(8,128)(2,1)S(1)} %copy-done.5, bf16[2,2,68,768]{3,2,1,0:T(8,128)(2,1)S(1)} %collective-permute-done.8.refs_0_, bf16[2,16,68,768]{3,2,1,0:T(8,128)(2,1)S(1)} %copy.30.refs_1_, bf16[2,16,68,768]{3,2,1,0:T(8,128)(2,1)S(1)} %copy-done.1, ...), custom_call_target="tpu_custom_call" | custom-call | flops 9814671360 | bytes 10862592 | tf_op jit(solution)/shard_map/pallas_call | solution.py:88
  205.6 23.3 %shard_map.84 = bf16[8,32,768]{2,1,0:T(8,128)(2,1)S(1)} custom-call(s32[1]{0:T(128)} %bitcast.29.dilation_ref, bf16[16,32,1536]{2,1,0:T(8,128)(2,1)S(1)} %copy-done.5, bf16[2,2,68,768]{3,2,1,0:T(8,128)(2,1)S(1)} %collective-permute-done.8.refs_0_, bf16[2,16,68,768]{3,2,1,0:T(8,128)(2,1)S(1)} %copy.30.refs_1_, bf16[2,16,68,768]{3,2,1,0:T(8,128)(2,1)S(1)} %copy-done.1, ...), custom_call_target="tpu_custom_call" | custom-call | flops 9814671360 | bytes 10862592 | tf_op jit(solution)/shard_map/pallas_call | solution.py:88
  228.9 2.3 fusion.23
  231.6 3.7 %fusion.17 = bf16[256,1536]{1,0:T(8,128)(2,1)S(1)} fusion(bf16[1536,3072]{1,0:T(8,128)(2,1)} %param.15, s32[]{:T(128)S(6)} %select_n.172, bf16[256,1536]{1,0:T(8,128)(2,1)S(1)} %collective-permute-done.12, bf16[256,768]{1,0:T(8,128)(2,1)S(1)} %bitcast.46, bf16[256,768]{1,0:T(8,128)(2,1)S(1)} %bitcast.50), kind=kOutput, calls=%fused_computation.13 | convolution fusion | flops 1210712064 | bytes 7077892 | tf_op jit(solution)/shard_map/dot_general | solution.py:210
  235.4 9.8 %collective-permute-done.13 = bf16[256,1536]{1,0:T(8,128)(2,1)} collective-permute-done((bf16[256,1536]{1,0:T(8,128)(2,1)}, bf16[256,1536]{1,0:T(8,128)(2,1)}, u32[]{:S(2)}, u32[]{:S(2)}) %collective-permute-start.13) | collective-permute-done | bytes 786464 | tf_op jit(solution)/shard_map/ppermute | solution.py:209
  245.2 3.9 %fusion.14 = bf16[256,1536]{1,0:T(8,128)(2,1)S(1)} fusion(bf16[1536,3072]{1,0:T(8,128)(2,1)} %param.15, s32[]{:T(128)S(6)} %select_n.172, bf16[256,1536]{1,0:T(8,128)(2,1)} %collective-permute-done.13, bf16[256,768]{1,0:T(8,128)(2,1)S(1)} %bitcast.44, bf16[256,768]{1,0:T(8,128)(2,1)S(1)} %bitcast.48), kind=kOutput, calls=%fused_computation.12 | convolution fusion | flops 1210712064 | bytes 7077892 | tf_op jit(solution)/shard_map/dot_general | solution.py:210
  (80 shorter events, 33.9 us)
Async XLA Ops:
  2.1 36.5 %copy-start.6 = (bf16[1,16,32,768]{3,2,1,0:T(8,128)(2,1)}, bf16[1,16,32,768]{3,2,1,0:T(8,128)(2,1)S(1)}, u32[]{:S(2)}) copy-start(bf16[1,16,32,768]{3,2,1,0:T(8,128)(2,1)S(1)} %get-tuple-element.14) | copy-start | bytes 2359300
  2.1 36.5 %copy-start.8 = (bf16[1,16,32,768]{3,2,1,0:T(8,128)(2,1)}, bf16[1,16,32,768]{3,2,1,0:T(8,128)(2,1)S(1)}, u32[]{:S(2)}) copy-start(bf16[1,16,32,768]{3,2,1,0:T(8,128)(2,1)S(1)} %get-tuple-element.19) | copy-start | bytes 2359300
  2.8 24.6 %collective-permute-start.1 = (bf16[2,16,18,768]{3,1,2,0:T(8,128)(2,1)S(1)}, bf16[2,16,18,768]{3,1,2,0:T(8,128)(2,1)S(1)}, u32[]{:S(2)}, u32[]{:S(2)}) collective-permute-start(bf16[2,16,18,768]{3,1,2,0:T(8,128)(2,1)S(1)} %copy.15), channel_id=1, source_target_pairs={{2,0},{4,2},{6,4},{3,1},{5,3},{7,5},{10,8},{12,10},{14,12},{11,9},... | collective-permute-start | bytes 2654216 | tf_op jit(solution)/shard_map/ppermute | solution.py:23
  4.2 24.5 %collective-permute-start = (bf16[2,16,18,768]{3,1,2,0:T(8,128)(2,1)S(1)}, bf16[2,16,18,768]{3,1,2,0:T(8,128)(2,1)S(1)}, u32[]{:S(2)}, u32[]{:S(2)}) collective-permute-start(bf16[2,16,18,768]{3,1,2,0:T(8,128)(2,1)S(1)} %copy.14), channel_id=1, source_target_pairs={{0,2},{2,4},{4,6},{1,3},{3,5},{5,7},{8,10},{10,12},{12,14},{9,11},... | collective-permute-start | bytes 2654216 | tf_op jit(solution)/shard_map/ppermute | solution.py:23
  32.4 48.7 %collective-permute-start.4 = (bf16[2,16,68,768]{3,1,2,0:T(8,128)(2,1)}, bf16[2,16,68,768]{3,1,2,0:T(8,128)(2,1)}, u32[]{:S(2)}, u32[]{:S(2)}) collective-permute-start(bf16[2,16,68,768]{3,1,2,0:T(8,128)(2,1)} %copy.18), channel_id=1, source_target_pairs={{8,0},{16,8},{24,16},{9,1},{17,9},{25,17},{10,2},{18,10},{26,18},{... | collective-permute-start | bytes 10027016 | tf_op jit(solution)/shard_map/ppermute | solution.py:23
  33.7 71.0 %collective-permute-start.3 = (bf16[2,16,68,768]{3,1,2,0:T(8,128)(2,1)}, bf16[2,16,68,768]{3,1,2,0:T(8,128)(2,1)}, u32[]{:S(2)}, u32[]{:S(2)}) collective-permute-start(bf16[2,16,68,768]{3,1,2,0:T(8,128)(2,1)} %copy.18), channel_id=1, source_target_pairs={{0,8},{8,16},{16,24},{1,9},{9,17},{17,25},{2,10},{10,18},{18,26},{... | collective-permute-start | bytes 10027016 | tf_op jit(solution)/shard_map/ppermute | solution.py:23
  40.2 24.0 %collective-permute-start.7 = (bf16[2,16,18,768]{3,1,2,0:T(8,128)(2,1)}, bf16[2,16,18,768]{3,1,2,0:T(8,128)(2,1)}, u32[]{:S(2)}, u32[]{:S(2)}) collective-permute-start(bf16[2,16,18,768]{3,1,2,0:T(8,128)(2,1)} %copy.25), channel_id=1, source_target_pairs={{2,0},{4,2},{6,4},{3,1},{5,3},{7,5},{10,8},{12,10},{14,12},{11,9},... | collective-permute-start | bytes 2654216 | tf_op jit(solution)/shard_map/ppermute | solution.py:23
  42.6 23.8 %collective-permute-start.6 = (bf16[2,16,18,768]{3,1,2,0:T(8,128)(2,1)}, bf16[2,16,18,768]{3,1,2,0:T(8,128)(2,1)}, u32[]{:S(2)}, u32[]{:S(2)}) collective-permute-start(bf16[2,16,18,768]{3,1,2,0:T(8,128)(2,1)} %copy.24), channel_id=1, source_target_pairs={{0,2},{2,4},{4,6},{1,3},{3,5},{5,7},{8,10},{10,12},{12,14},{9,11},... | collective-permute-start | bytes 2654216 | tf_op jit(solution)/shard_map/ppermute | solution.py:23
  68.9 18.4 %copy-start.10 = (f32[24,13,13]{0,2,1:T(8,128)S(1)}, f32[24,13,13]{0,2,1:T(8,128)}, u32[]{:S(2)}) copy-start(f32[24,13,13]{0,2,1:T(8,128)} %param.14) | copy-start | bytes 48676
  71.7 99.1 %collective-permute-start.10 = (bf16[2,16,68,768]{3,1,2,0:T(8,128)(2,1)}, bf16[2,16,68,768]{3,1,2,0:T(8,128)(2,1)}, u32[]{:S(2)}, u32[]{:S(2)}) collective-permute-start(bf16[2,16,68,768]{3,1,2,0:T(8,128)(2,1)} %copy.28), channel_id=1, source_target_pairs={{8,0},{16,8},{24,16},{9,1},{17,9},{25,17},{10,2},{18,10},{26,18},{... | collective-permute-start | bytes 10027016 | tf_op jit(solution)/shard_map/ppermute | solution.py:23
  73.0 102.7 %collective-permute-start.9 = (bf16[2,16,68,768]{3,1,2,0:T(8,128)(2,1)}, bf16[2,16,68,768]{3,1,2,0:T(8,128)(2,1)}, u32[]{:S(2)}, u32[]{:S(2)}) collective-permute-start(bf16[2,16,68,768]{3,1,2,0:T(8,128)(2,1)} %copy.28), channel_id=1, source_target_pairs={{0,8},{8,16},{16,24},{1,9},{9,17},{17,25},{2,10},{10,18},{18,26},{... | collective-permute-start | bytes 10027016 | tf_op jit(solution)/shard_map/ppermute | solution.py:23
  79.8 47.1 %collective-permute-start.5 = (bf16[2,2,68,768]{3,2,1,0:T(8,128)(2,1)}, bf16[2,2,68,768]{3,2,1,0:T(8,128)(2,1)}, u32[]{:S(2)}, u32[]{:S(2)}) collective-permute-start(bf16[2,2,68,768]{3,2,1,0:T(8,128)(2,1)} %get-tuple-element.5), channel_id=1, source_target_pairs={{16,0},{24,8},{17,1},{25,9},{18,2},{26,10},{19,3},{27,11},{20,4},{... | collective-permute-start | bytes 1253384 | tf_op jit(solution)/shard_map/ppermute | solution.py:23
  81.1 47.4 %collective-permute-start.2 = (bf16[2,2,68,768]{3,2,1,0:T(8,128)(2,1)}, bf16[2,2,68,768]{3,2,1,0:T(8,128)(2,1)}, u32[]{:S(2)}, u32[]{:S(2)}) collective-permute-start(bf16[2,2,68,768]{3,2,1,0:T(8,128)(2,1)} %get-tuple-element.6), channel_id=1, source_target_pairs={{0,16},{8,24},{1,17},{9,25},{2,18},{10,26},{3,19},{11,27},{4,20},{... | collective-permute-start | bytes 1253384 | tf_op jit(solution)/shard_map/ppermute | solution.py:23
  104.7 23.9 %copy-start.2 = (f32[24,13,1040]{2,1,0:T(8,128)S(1)}, f32[24,13,1040]{2,1,0:T(8,128)}, u32[]{:S(2)}) copy-start(f32[24,13,1040]{2,1,0:T(8,128)} %copy.23.refs_6_) | copy-start | bytes 3893764
  104.7 23.9 %copy-start.3 = (s32[32,1040]{1,0:T(8,128)S(1)}, s32[32,1040]{1,0:T(8,128)}, u32[]{:S(2)}) copy-start(s32[32,1040]{1,0:T(8,128)} %select_select_fusion.1.refs_5_) | copy-start | bytes 399364
  104.7 23.9 %copy-start.4 = (f32[16,1040]{1,0:T(8,128)S(1)}, f32[16,1040]{1,0:T(8,128)}, u32[]{:S(2)}) copy-start(f32[16,1040]{1,0:T(8,128)} %fusion.34.refs_7_) | copy-start | bytes 199684
  104.7 23.9 %copy-start.5 = (bf16[16,32,1536]{2,1,0:T(8,128)(2,1)S(1)}, bf16[16,32,1536]{2,1,0:T(8,128)(2,1)}, u32[]{:S(2)}) copy-start(bf16[16,32,1536]{2,1,0:T(8,128)(2,1)} %q_ref.5) | copy-start | bytes 4718596
  104.7 74.3 %collective-permute-start.11 = (bf16[2,2,68,768]{3,2,1,0:T(8,128)(2,1)S(1)}, bf16[2,2,68,768]{3,2,1,0:T(8,128)(2,1)S(1)}, u32[]{:S(2)}, u32[]{:S(2)}) collective-permute-start(bf16[2,2,68,768]{3,2,1,0:T(8,128)(2,1)S(1)} %get-tuple-element.7), channel_id=1, source_target_pairs={{16,0},{24,8},{17,1},{25,9},{18,2},{26,10},{19,3},{27,11},{20,4},{... | collective-permute-start | bytes 1253384 | tf_op jit(solution)/shard_map/ppermute | solution.py:23
  126.9 52.1 %collective-permute-start.8 = (bf16[2,2,68,768]{3,2,1,0:T(8,128)(2,1)S(1)}, bf16[2,2,68,768]{3,2,1,0:T(8,128)(2,1)S(1)}, u32[]{:S(2)}, u32[]{:S(2)}) collective-permute-start(bf16[2,2,68,768]{3,2,1,0:T(8,128)(2,1)S(1)} %get-tuple-element.8), channel_id=1, source_target_pairs={{0,16},{8,24},{1,17},{9,25},{2,18},{10,26},{3,19},{11,27},{4,20},{... | collective-permute-start | bytes 1253384 | tf_op jit(solution)/shard_map/ppermute | solution.py:23
  175.7 26.8 %slice-start = ((s8[9437184]{0:T(1024)(128)(4,1)}), s8[1048576]{0:T(1024)(128)(4,1)S(1)}, s32[]{:S(2)}) async-start(s8[9437184]{0:T(1024)(128)(4,1)} %bitcast.51), calls=%async_computation | async-start | bytes 2097152
  179.0 23.5 %slice-start.1 = ((s8[9437184]{0:T(1024)(128)(4,1)}), s8[4194304]{0:T(1024)(128)(4,1)S(1)}, s32[]{:S(2)}) async-start(s8[9437184]{0:T(1024)(128)(4,1)} %bitcast.51), calls=%async_computation.1 | async-start | bytes 8388608
  179.0 23.5 %slice-start.2 = ((s8[9437184]{0:T(1024)(128)(4,1)}), s8[4194304]{0:T(1024)(128)(4,1)S(1)}, s32[]{:S(2)}) async-start(s8[9437184]{0:T(1024)(128)(4,1)} %bitcast.51), calls=%async_computation.2 | async-start | bytes 8388608
  203.9 27.7 %collective-permute-start.12 = (bf16[256,1536]{1,0:T(8,128)(2,1)S(1)}, bf16[256,1536]{1,0:T(8,128)(2,1)S(1)}, u32[]{:S(2)}, u32[]{:S(2)}) collective-permute-start(bf16[256,1536]{1,0:T(8,128)(2,1)S(1)} %fusion.20), channel_id=1, source_target_pairs={{0,1},{1,0},{2,3},{3,2},{4,5},{5,4},{6,7},{7,6},{8,9},{9,8},{10,11... | collective-permute-start | bytes 2359304 | tf_op jit(solution)/shard_map/ppermute | solution.py:209
  231.1 14.0 %collective-permute-start.13 = (bf16[256,1536]{1,0:T(8,128)(2,1)}, bf16[256,1536]{1,0:T(8,128)(2,1)}, u32[]{:S(2)}, u32[]{:S(2)}) collective-permute-start(bf16[256,1536]{1,0:T(8,128)(2,1)} %fusion.23), channel_id=1, source_target_pairs={{0,1},{1,0},{2,3},{3,2},{4,5},{5,4},{6,7},{7,6},{8,9},{9,8},{10,11... | collective-permute-start | bytes 2359304 | tf_op jit(solution)/shard_map/ppermute | solution.py:209
  (5 other events, 53.0 us)
